TPU v7x, 256 devices: a whole 4x4x8 slice. The times are simulated.
256 devices in a mesh: tp: 4 (over x), rep: 64 (over y, z, core).
Axes of the slice: x: 4, y: 4, z: 8, core: 2. Of those that a mesh axis runs over, the one named last changes fastest.
Arguments:
- queries: bfloat16 [1024, 4096], P('rep', 'tp'), may hold values from -6 to 6
- new_keys: bfloat16 [1024, 2048], P('rep', 'tp'), may hold values from -6 to 6
- new_values: bfloat16 [1024, 2048], P('rep', 'tp'), may hold values from -6 to 6
- stored_keys: bfloat16 [1024, 16, 128, 128], P('rep', 'tp'), may hold values from -6 to 6
- stored_values: bfloat16 [1024, 16, 128, 128], P('rep', 'tp'), may hold values from -6 to 6
- lengths: int32 [1024], P('rep'), may hold values from 1 to 128
- out_proj: bfloat16 [4096, 4608], P('tp', 'rep'), may hold values from -0.09375 to 0.09375
- residual: bfloat16 [1024, 4608], P(None, 'rep'), may hold values from -4.5 to 4.5
- norm_gain: float32 [4608], replicated, may hold values from 0.1 to 1.9
- embedding: bfloat16 [256000, 4608], P(('tp', 'rep')), may hold values from -1.25 to 1.25
- targets: int32 [1024], replicated, may hold values from 0 to 255999
- old_sums: float32 [1024], P('rep'), may hold values from -3 to 0
- rewards: float32 [1024], P('rep'), may hold values from -6 to 6
- group_ids: int32 [1024], P('rep'), may hold values from 0 to 127, as said below
Outputs:
- logprob_sum: float32 [1024], P('rep')
- advantage: float32 [1024], P('rep')
Inputs may be any that keep to these rules, and one draw needn't show every extreme that they name: `group_ids`: each id names exactly 8 continuations.
All inputs are finite; a program needn't handle non-finite values.
Results may differ from a plain program's by a relative error of at most 0.001.
Values may be sent and summed in bfloat16 or wider, within the bound.
No kernel may reach another device: no remote copies, remote signals or barrier semaphores. Data moves between devices by JAX's collectives and lax.ppermute only.
A program may use at most 64 MiB of HBM per device.

v0:
```python
import jax
import jax.numpy as jnp
from jax import lax
from jax.sharding import Mesh
from jax.sharding import PartitionSpec as P

D = 4608
GROUP = 8
REP = ("rep_0", "rep_1", "rep_2")
TP_REP = ("tp", "rep_0", "rep_1", "rep_2")


def sent_to_all(x, axis):
    devices = lax.axis_size(axis)
    return lax.all_to_all(jnp.broadcast_to(x[None], (devices, *x.shape)), axis, 0, 0, tiled=True)


def of_everyone(x, axis):
    everything = sent_to_all(x, axis)
    return jnp.sum(everything, axis=0)


def laid_out(blocks, dim):
    lengths = list(blocks.shape[1:])
    lengths[dim] *= blocks.shape[0]
    return jnp.moveaxis(blocks, 0, dim).reshape(lengths)


def whole_of(x, axes, dim):
    far, near = axes
    blocks = sent_to_all(sent_to_all(x, far), near)
    return laid_out(blocks.swapaxes(0, 1).reshape(-1, *x.shape), dim)


def over_axes(x, axes):
    far, near = axes
    nearer = of_everyone(x, near)
    return of_everyone(nearer, far)


def packed_total(arrays, axis):
    ravelled, at, finished = (jnp.concatenate([a.reshape(-1) for a in arrays]), 0, [])
    subtotal = over_axes(ravelled, axis)
    for a in arrays:
        finished.append(subtotal[at : at + a.size].reshape(a.shape))
        at += a.size
    return tuple(finished)


def attention(queries, new_keys, new_values, stored_keys, stored_values, lengths):
    samp, heads_kv, span, depth = stored_keys.shape
    sample_ratio = queries.shape[1] // (heads_kv * depth)
    query_vector = queries.reshape(samp, heads_kv, sample_ratio, depth)
    scores = (
        jnp.einsum("sgqd,sgpd->sgqp", query_vector, stored_keys, preferred_element_type=jnp.float32)
        / 12.0
    )
    scores = 50.0 * jnp.tanh(scores / 50.0)
    valid = lax.broadcasted_iota(jnp.int32, (samp, 1, 1, span), 3) < lengths[:, None, None, None]
    expo = jnp.where(valid, jnp.exp(scores), 0.0)
    own_logit = (
        jnp.einsum(
            "sgqd,sgd->sgq",
            query_vector,
            new_keys.reshape(samp, heads_kv, depth),
            preferred_element_type=jnp.float32,
        )
        / 12.0
    )
    own_logit = 50.0 * jnp.tanh(own_logit / 50.0)
    own_exp = jnp.exp(own_logit)
    total = jnp.sum(expo, -1) + own_exp
    probs = (expo / total[..., None]).astype(jnp.bfloat16)
    own_probability = (own_exp / total).astype(jnp.bfloat16)
    attended_output = jnp.einsum(
        "sgqp,sgpd->sgqd", probs, stored_values, preferred_element_type=jnp.float32
    )
    attended_output = attended_output + own_probability.astype(jnp.float32)[
        ..., None
    ] * new_values.reshape(samp, heads_kv, 1, depth).astype(jnp.float32)
    return attended_output.reshape(samp, sample_ratio * heads_kv * depth).astype(jnp.bfloat16)


def per_device(
    queries,
    new_keys,
    new_values,
    stored_keys,
    stored_values,
    lengths,
    out_proj,
    residual,
    norm_gain,
    embedding,
    targets,
    old_sums,
    rewards,
    group_ids,
):
    samp = queries.shape[0]
    reps = lax.axis_size(REP)
    rep_index = lax.axis_index(REP)
    tp_index = lax.axis_index("tp")
    groups = samp * reps // GROUP
    member = group_ids[:, None] == lax.broadcasted_iota(jnp.int32, (1, groups), 1)
    reward_part = jnp.sum(jnp.where(member, rewards[:, None], 0.0), 0)
    group_total = of_everyone(reward_part, REP)
    mine = jnp.sum(jnp.where(member, group_total[None, :], 0.0), 1)
    advantage = rewards - (mine - rewards) / (GROUP - 1.0)
    context = attention(queries, new_keys, new_values, stored_keys, stored_values, lengths)
    partial_value = jnp.dot(
        whole_of(context, (("rep_0", "rep_1"), "rep_2"), 0),
        out_proj,
        preferred_element_type=jnp.float32,
    )
    columns = residual.shape[1]
    vocab_rows = embedding.shape[0]
    contract = (((1,), (1,)), ((), ()))
    heads = of_everyone(partial_value, "tp")
    stream = residual.astype(jnp.float32) + heads
    squares = of_everyone(jnp.sum(stream * stream, 1), REP)
    scale = lax.rsqrt(squares / D + 1e-06)
    gain_part = lax.dynamic_slice_in_dim(norm_gain, rep_index * columns, columns)
    normed = (stream * scale[:, None] * gain_part[None, :]).astype(jnp.bfloat16)
    gathered = lax.all_gather(normed, REP, axis=1, tiled=True)
    logits = lax.dot_general(gathered, embedding, contract, preferred_element_type=jnp.float32)
    capped = 30.0 * jnp.tanh(logits / 30.0)
    offset = (tp_index * reps + rep_index) * vocab_rows
    entry_ids = offset + lax.broadcasted_iota(jnp.int32, (1, vocab_rows), 1)
    picked_part = jnp.sum(jnp.where(entry_ids == targets[:, None], capped, 0.0), 1)
    total, picked = packed_total(
        (jnp.sum(jnp.exp(capped), 1), picked_part), (("tp", "rep_0"), ("rep_1", "rep_2"))
    )
    logprob = picked - jnp.log(total)
    own_rows = lax.dynamic_slice_in_dim(logprob, rep_index * samp, samp)
    logprob_sum = old_sums + own_rows
    return (logprob_sum, advantage)


def solution(mesh):
    split = Mesh(mesh.devices.reshape(mesh.shape["tp"], 4, 8, 2), ("tp", "rep_0", "rep_1", "rep_2"))
    placed = (
        P(REP, "tp"),
        P(REP, "tp"),
        P(REP, "tp"),
        P(REP, "tp", None, None),
        P(REP, "tp", None, None),
        P(REP),
        P("tp", REP),
        P(None, REP),
        P(),
        P(TP_REP, None),
        P(),
        P(REP),
        P(REP),
        P(REP),
    )
    return jax.shard_map(
        per_device, mesh=split, in_specs=placed, out_specs=(P(REP), P(REP)), check_vma=False
    )
```

profile of v0, /device:TPU:1, one launch (start us, length us, event | category | flops | bytes accessed | tf_op | source)
XLA Modules:
  0.0 235.7 jit_solution(11303239664290411377)
XLA Ops:
  7.2 0.9 reshape.88
  8.1 0.7 iota_compare_fusion.1
  8.8 1.3 fusion.12
  10.2 0.7 reshape.94
  11.5 0.7 reshape.90
  12.3 2.3 fusion.4
  14.7 36.7 %all_to_all.39 = bf16[32,16,1024]{2,1,0:T(8,128)(2,1)S(1)} all-to-all(bf16[32,16,1024]{2,1,0:T(8,128)(2,1)S(1)} %broadcast_in_dim.53), channel_id=1, replica_groups=mesh['tp'=4,'rep_0'=4,'rep_1'=8,'rep_2'=2] {'rep_0','rep_1'}, dimensions={0} | all-to-all | bytes 2097152 | tf_op jit(solution)/shard_map/all_to_all | solution.py:15
  51.7 9.9 %all_to_all.40 = bf16[2,32,16,1024]{3,2,1,0:T(8,128)(2,1)S(1)} all-to-all(bf16[2,32,16,1024]{3,2,1,0:T(8,128)(2,1)S(1)} %broadcast_in_dim.55), channel_id=1, replica_groups=mesh['tp'=4,'rep_0'=4,'rep_1'=8,'rep_2'=2] {'rep_2'}, dimensions={0} | all-to-all | bytes 4194304 | tf_op jit(solution)/shard_map/all_to_all | solution.py:15
  61.9 0.8 fusion.14
  62.9 19.5 %all_to_all.41 = f32[4,1024,72]{1,2,0:T(8,128)S(1)} all-to-all(f32[4,1024,72]{1,2,0:T(8,128)S(1)} %broadcast_in_dim.56), channel_id=1, replica_groups=mesh['tp'=4,'rep_0'=4,'rep_1'=8,'rep_2'=2] {'tp'}, dimensions={0} | all-to-all | bytes 2359296 | tf_op jit(solution)/shard_map/all_to_all | solution.py:15
  82.3 0.8 reduce_sum.100
  83.1 1.0 multiply_reduce_fusion
  84.2 0.8 broadcast_in_dim.57
  85.0 7.1 %all-to-all-start.3 = ((f32[64,1,1024]{2,1,0:T(1,128)}), f32[64,1,1024]{2,1,0:T(1,128)S(1)}, u32[]{:S(2)}, u32[]{:S(2)}) async-start(f32[64,1,1024]{2,1,0:T(1,128)} %broadcast_in_dim.57), calls=%async_computation.3 | async-start | bytes 524288 | tf_op jit(solution)/shard_map/all_to_all | solution.py:15
  92.1 0.8 dynamic_slice.6
  92.9 11.1 %all-to-all-done.3 = f32[64,1,1024]{2,1,0:T(1,128)S(1)} async-done(((f32[64,1,1024]{2,1,0:T(1,128)}), f32[64,1,1024]{2,1,0:T(1,128)S(1)}, u32[]{:S(2)}, u32[]{:S(2)}) %all-to-all-start.3) | async-done | bytes 262176 | tf_op jit(solution)/shard_map/all_to_all | solution.py:15
  104.2 1.7 multiply_convert_fusion
  106.7 6.0 %all-to-all-start.6 = ((f32[64,1,128]{2,1,0:T(1,128)}), f32[64,1,128]{2,1,0:T(1,128)S(1)}, u32[]{:S(2)}, u32[]{:S(2)}) async-start(f32[64,1,128]{2,1,0:T(1,128)} %broadcast_in_dim.100), calls=%async_computation.6 | async-start | bytes 65536 | tf_op jit(solution)/shard_map/all_to_all | solution.py:15
  112.8 72.8 %all-gather.2.cloned.1.call-done = bf16[1024,4608]{0,1:T(8,128)(2,1)} async-done(((bf16[1024,72]{0,1:T(8,128)(2,1)}), bf16[1024,4608]{0,1:T(8,128)(2,1)}) %all-gather.2.cloned.1.call-update) | async-done | bytes 9437200 | tf_op jit(solution)/shard_map/all_gather | solution.py:125
  185.6 15.7 %exponential_reduce_fusion = (f32[1024]{0:T(1024)S(1)}, f32[1024]{0:T(1024)S(1)}) fusion(s32[1024]{0:T(1024)S(1)} %copy-done.4, s32[1000]{0:T(1024)S(1)} %iota_add_fusion, bf16[1024,4608]{0,1:T(8,128)(2,1)} %all-gather.2.cloned.1.call-done, bf16[1000,4608]{1,0:T(8,128)(2,1)} %param.23), kind=kOutput, calls=%fused_computation.1 | convolution fusion | flops 9443325952 | bytes 18669472 | tf_op jit(solution)/shard_map/dot_general | solution.py:126
  202.1 4.7 %all-to-all-start.4 = ((f32[16,1,2048]{2,1,0:T(1,128)}), f32[16,1,2048]{2,1,0:T(1,128)S(1)}, u32[]{:S(2)}, u32[]{:S(2)}) async-start(f32[16,1,2048]{2,1,0:T(1,128)} %broadcast_in_dim.59), calls=%async_computation.4 | async-start | bytes 262144 | tf_op jit(solution)/shard_map/all_to_all | solution.py:15
  206.9 8.7 %all-to-all-done.4 = f32[16,1,2048]{2,1,0:T(1,128)S(1)} async-done(((f32[16,1,2048]{2,1,0:T(1,128)}), f32[16,1,2048]{2,1,0:T(1,128)S(1)}, u32[]{:S(2)}, u32[]{:S(2)}) %all-to-all-start.4) | async-done | bytes 131104 | tf_op jit(solution)/shard_map/all_to_all | solution.py:15
  216.4 5.0 %all-to-all-start.5 = ((f32[16,1,2048]{2,1,0:T(1,128)}), f32[16,1,2048]{2,1,0:T(1,128)S(1)}, u32[]{:S(2)}, u32[]{:S(2)}) async-start(f32[16,1,2048]{2,1,0:T(1,128)} %broadcast_in_dim.60), calls=%async_computation.5 | async-start | bytes 262144 | tf_op jit(solution)/shard_map/all_to_all | solution.py:15
  221.9 6.3 %all-to-all-done.5 = f32[16,1,2048]{2,1,0:T(1,128)S(1)} async-done(((f32[16,1,2048]{2,1,0:T(1,128)}), f32[16,1,2048]{2,1,0:T(1,128)S(1)}, u32[]{:S(2)}, u32[]{:S(2)}) %all-to-all-start.5) | async-done | bytes 131104 | tf_op jit(solution)/shard_map/all_to_all | solution.py:15
  (43 shorter events, 5.4 us)
Async XLA Ops:
  7.2 1.7 copy-start
  51.7 10.2 %copy-start.2 = (bf16[1024,72]{0,1:T(8,128)(2,1)S(1)}, bf16[1024,72]{0,1:T(8,128)(2,1)}, u32[]{:S(2)}) copy-start(bf16[1024,72]{0,1:T(8,128)(2,1)} %param.20) | copy-start | bytes 442372
  61.9 21.2 %copy-start.1 = (bf16[1024,72]{0,1:T(8,128)(2,1)S(1)}, bf16[1024,72]{0,1:T(8,128)(2,1)}, u32[]{:S(2)}) copy-start(bf16[1024,72]{0,1:T(8,128)(2,1)} %param.21) | copy-start | bytes 442372
  62.7 43.2 %copy-start.5 = (s32[16]{0:T(128)S(1)}, s32[16]{0:T(128)}, u32[]{:S(2)}) copy-start(s32[16]{0:T(128)} %param.27) | copy-start | bytes 196
  62.7 43.2 %copy-start.6 = (f32[16]{0:T(128)S(1)}, f32[16]{0:T(128)}, u32[]{:S(2)}) copy-start(f32[16]{0:T(128)} %param.26) | copy-start | bytes 196
  62.7 122.9 %copy-start.4 = (s32[1024]{0:T(1024)S(1)}, s32[1024]{0:T(1024)}, u32[]{:S(2)}) copy-start(s32[1024]{0:T(1024)} %param.24) | copy-start | bytes 12292
  85.0 19.0 %all-to-all-start.3 = ((f32[64,1,1024]{2,1,0:T(1,128)}), f32[64,1,1024]{2,1,0:T(1,128)S(1)}, u32[]{:S(2)}, u32[]{:S(2)}) async-start(f32[64,1,1024]{2,1,0:T(1,128)} %broadcast_in_dim.57), calls=%async_computation.3 | async-start | bytes 524288 | tf_op jit(solution)/shard_map/all_to_all | solution.py:15
  92.0 93.6 %all-gather.2.cloned.1.call-start = ((), (), s32[]{:S(2)}) async-start(), calls=%async_computation.7 | async-start | bytes 9584640 | tf_op jit(solution)/shard_map/all_gather | solution.py:125
  106.7 94.7 %all-to-all-start.6 = ((f32[64,1,128]{2,1,0:T(1,128)}), f32[64,1,128]{2,1,0:T(1,128)S(1)}, u32[]{:S(2)}, u32[]{:S(2)}) async-start(f32[64,1,128]{2,1,0:T(1,128)} %broadcast_in_dim.100), calls=%async_computation.6 | async-start | bytes 65536 | tf_op jit(solution)/shard_map/all_to_all | solution.py:15
  112.7 115.5 %copy-start.3 = (f32[16]{0:T(128)S(1)}, f32[16]{0:T(128)}, u32[]{:S(2)}) copy-start(f32[16]{0:T(128)} %param.25) | copy-start | bytes 196
  202.1 13.5 %all-to-all-start.4 = ((f32[16,1,2048]{2,1,0:T(1,128)}), f32[16,1,2048]{2,1,0:T(1,128)S(1)}, u32[]{:S(2)}, u32[]{:S(2)}) async-start(f32[16,1,2048]{2,1,0:T(1,128)} %broadcast_in_dim.59), calls=%async_computation.4 | async-start | bytes 262144 | tf_op jit(solution)/shard_map/all_to_all | solution.py:15
  216.4 11.7 %all-to-all-start.5 = ((f32[16,1,2048]{2,1,0:T(1,128)}), f32[16,1,2048]{2,1,0:T(1,128)S(1)}, u32[]{:S(2)}, u32[]{:S(2)}) async-start(f32[16,1,2048]{2,1,0:T(1,128)} %broadcast_in_dim.60), calls=%async_computation.5 | async-start | bytes 262144 | tf_op jit(solution)/shard_map/all_to_all | solution.py:15
Sparse Core Ops, SparseCore 0:
  106.1 79.4 all-gather.1
where the time goes:
time: 237 us; the launch traced here: 236 us
  waiting for transfers between devices  98.9 us (42%)
  blocking collectives  66 us (28%)
  starting transfers between devices  22.8 us (10%)
  matrix products  20.3 us (9%)
  between operations  14.3 us (6%)
  local copies, waits for them, and re-layouts  7.36 us (3%)
  other arithmetic  6.06 us (3%)
    all_gather x1, waiting for transfers between devices, per_device(): gathered = lax.all_gather(normed, REP, axis=1, tiled=True)  72.8 us
    all_to_all x3, blocking collectives, sent_to_all(): lax.all_to_all(jnp.broadcast_to(x[None], (devices, *x.shape)), axis, 0, 0...  66 us
    all_to_all x4, waiting for transfers between devices, sent_to_all(): lax.all_to_all(jnp.broadcast_to(x[None], (devices, *x.shape)), axis, 0, 0...  26.1 us
    all_to_all x4, starting transfers between devices, sent_to_all(): lax.all_to_all(jnp.broadcast_to(x[None], (devices, *x.shape)), axis, 0, 0...  22.7 us
    dot_general x1, matrix products, per_device(): lax.dot_general(gathered, embedding, contract, preferred_element_type=jnp...  15.7 us
  transfers between devices with their start and end apart: 5, of which 4 were waited for; matrix products, arithmetic and copies ran while one was open for 8% of the time, Pallas kernels for 0%

commit v1 on v0

v1 whole, which is shorter than its diff:
```python
import functools

import jax
import jax.numpy as jnp
from jax import lax
from jax.experimental import pallas as pl
from jax.experimental.pallas import tpu as pltpu
from jax.sharding import Mesh
from jax.sharding import PartitionSpec as P

D = 4608
GROUP = 8
REP = ("y", "z", "c")
TP_REP = ("x", "y", "z", "c")
BF16 = jnp.bfloat16
F32 = jnp.float32


def shifted(x, axis, offset):
    n = lax.axis_size(axis)
    return lax.ppermute(x, axis, [((i + offset) % n, i) for i in range(n)])


def rolled(x, start, dim):
    n = x.shape[dim]
    return lax.dynamic_slice_in_dim(jnp.concatenate([x, x], dim), start, n, dim)


NT = (((1,), (1,)), ((), ()))
VMEM = pl.BlockSpec(memory_space=pltpu.VMEM)
SMEM = pl.BlockSpec(memory_space=pltpu.SMEM)


def attention_kernel(
    lengths_ref, q_ref, nk_ref, nv_ref, k_hbm, v_hbm, out_ref, k_ref, v_ref, k_sem, v_sem
):
    kv, samp, span, depth = k_ref.shape
    copies, ratio = out_ref.shape[0], q_ref.shape[1] // (kv * depth)
    k_copy = [pltpu.make_async_copy(k_hbm.at[:, g], k_ref.at[g], k_sem.at[g]) for g in range(kv)]
    v_copy = [pltpu.make_async_copy(v_hbm.at[:, g], v_ref.at[g], v_sem.at[g]) for g in range(kv)]
    for g in range(kv):
        k_copy[g].start()
        v_copy[g].start()
    row = lax.broadcasted_iota(jnp.int32, (ratio * samp, span), 0)
    slot = lax.broadcasted_iota(jnp.int32, (ratio * samp, span), 1)
    sample = lax.rem(row, samp)
    live = jnp.concatenate([lengths_ref[...]] * ratio, 0)
    for g in range(kv):
        heads = [pl.ds((g * ratio + r) * depth, depth) for r in range(ratio)]
        q = jnp.concatenate([q_ref[:, h].astype(F32) for h in heads], 0)
        q16 = q.astype(BF16)
        nk = jnp.concatenate([nk_ref[:, pl.ds(g * depth, depth)].astype(F32)] * ratio, 0)
        nv = jnp.concatenate([nv_ref[:, pl.ds(g * depth, depth)].astype(F32)] * ratio, 0)
        k_copy[g].wait()
        scores = jnp.zeros((ratio * samp, span), F32)
        for s in range(samp):
            found = lax.dot_general(q16, k_ref[g, s], NT, preferred_element_type=F32)
            scores = jnp.where(sample == s, found, scores)
        scores = 50.0 * jnp.tanh(scores / 12.0 / 50.0)
        expo = jnp.where(slot < live, jnp.exp(scores), 0.0)
        own = jnp.sum(q * nk, 1, keepdims=True)
        own = jnp.exp(50.0 * jnp.tanh(own / 12.0 / 50.0))
        total = jnp.sum(expo, 1, keepdims=True) + own
        probs = (expo / total).astype(BF16)
        own_prob = (own / total).astype(BF16).astype(F32)
        v_copy[g].wait()
        out = own_prob * nv
        found = jnp.zeros_like(out)
        for s in range(samp):
            one = jnp.dot(probs, v_ref[g, s], preferred_element_type=F32)
            found = jnp.where(sample == s, one, found)
        out = (found + out).astype(BF16)
        for r in range(ratio):
            for i in range(copies):
                out_ref[i, :, heads[r]] = out[r * samp : (r + 1) * samp]


def attention(queries, new_keys, new_values, stored_keys, stored_values, lengths, copies):
    samp, kv, span, depth = stored_keys.shape
    hbm = pl.BlockSpec(memory_space=pltpu.HBM)
    return pl.pallas_call(
        attention_kernel,
        out_shape=jax.ShapeDtypeStruct((copies, *queries.shape), BF16),
        in_specs=[VMEM, VMEM, VMEM, VMEM, hbm, hbm],
        out_specs=VMEM,
        scratch_shapes=[
            pltpu.VMEM((kv, samp, span, depth), BF16),
            pltpu.VMEM((kv, samp, span, depth), BF16),
            pltpu.SemaphoreType.DMA((kv,)),
            pltpu.SemaphoreType.DMA((kv,)),
        ],
        compiler_params=pltpu.CompilerParams(vmem_limit_bytes=58 << 20),
        cost_estimate=pl.CostEstimate(
            flops=4 << 30, bytes_accessed=4 << 20, transcendentals=1 << 16
        ),
        name="attend",
    )(lengths.reshape(samp, 1), queries, new_keys, new_values, stored_keys, stored_values)


def stream_kernel(at_ref, a_ref, b_ref, c_ref, d_ref, res_ref, gain_ref, out_ref, *, samp):
    rows, _ = a_ref.shape
    heads = (a_ref[...] + b_ref[...]) + (c_ref[...] + d_ref[...])
    res = jnp.concatenate([res_ref[i].astype(F32) for i in range(res_ref.shape[0])], 0).T
    half = res.shape[0] // 2
    res = jnp.where(at_ref[0] == 0, res[:half], res[half:])
    cores = half // rows
    units = []
    for u in range(rows // samp):
        at = u * cores * samp
        units.append(jnp.where(at_ref[1] == 0, res[at : at + samp], res[at + samp : at + 2 * samp]))
    value = ((heads + jnp.concatenate(units, 0)) * gain_ref[...]).astype(BF16)
    for i in range(out_ref.shape[0]):
        out_ref[i] = value


def assemble_kernel(got_ref, inverse_ref, out_ref, *, ny):
    nz, rows, wide = got_ref.shape
    width = wide // ny
    got = [got_ref[k].astype(F32) for k in range(nz)]
    pieces = [got[k][:, j * width : (j + 1) * width] for j in range(ny) for k in range(nz)]
    whole = jnp.concatenate(pieces, 1)
    out_ref[:, :D] = whole.astype(BF16)
    plain = whole * inverse_ref[...]
    scale = lax.rsqrt(jnp.sum(plain * plain, 1, keepdims=True) * (1.0 / D) + 1e-06) * (1.0 / 30.0)
    high = scale.astype(BF16).astype(F32)
    middle = (scale - high).astype(BF16).astype(F32)
    low = scale - high - middle
    lane = lax.broadcasted_iota(jnp.int32, (rows, out_ref.shape[1] - D), 1)
    tail = jnp.where(lane == 0, high, jnp.where(lane == 1, middle, jnp.where(lane == 2, low, 0.0)))
    out_ref[:, D:] = tail.astype(BF16)


def loss_kernel(*refs, blocks):
    base_ref, mark_ref, ready_ref, table_hbm = refs[:4]
    pieces = refs[4 : 4 + blocks]
    out_ref, rows_ref, table_ref, sem = refs[4 + blocks :]
    vocab = table_ref.shape[0]
    cuts = [*range(0, vocab, 512), vocab]
    parts = list(zip(cuts[:-1], cuts[1:]))
    copies = []
    for i, (lo, hi) in enumerate(parts):
        part = pl.ds(lo, hi - lo)
        copies.append(pltpu.make_async_copy(table_hbm.at[part], table_ref.at[part], sem.at[i]))
        copies[i].start()
    rows = 0
    for piece in pieces:
        rows_ref[rows : rows + piece.shape[0]] = piece[...]
        rows += piece.shape[0]
    scale = jnp.sum(rows_ref[:, D:].astype(F32), 1, keepdims=True)
    mark = mark_ref[...]
    total = jnp.zeros((rows, 1), F32)
    picked = jnp.zeros((rows, 1), F32)
    for which, ref in enumerate((ready_ref, table_ref)):
        for i, (lo, hi) in enumerate(parts):
            if which:
                copies[i].wait()
            acc = lax.dot_general(rows_ref[:, :D], ref[lo:hi], NT, preferred_element_type=F32)
            logits = 30.0 * jnp.tanh(acc * scale)
            ids = base_ref[1 - which] + lo + lax.broadcasted_iota(jnp.int32, (1, hi - lo), 1)
            total += jnp.sum(jnp.exp(logits), 1, keepdims=True)
            picked += jnp.sum(jnp.where(ids == mark, logits, 0.0), 1, keepdims=True)
    lane = lax.broadcasted_iota(jnp.int32, (rows, 128), 1)
    both = jnp.where(lane == 0, total, jnp.where(lane == 1, picked, 0.0))
    out_ref[...] = both.T[:8]


def losses(pieces, mark, tables, bases):
    rows = sum(p.shape[0] for p in pieces)
    vocab = tables[0].shape[0]
    return pl.pallas_call(
        functools.partial(loss_kernel, blocks=len(pieces)),
        out_shape=jax.ShapeDtypeStruct((8, rows), F32),
        in_specs=[SMEM, VMEM, VMEM, pl.BlockSpec(memory_space=pltpu.HBM)] + [VMEM] * len(pieces),
        out_specs=VMEM,
        scratch_shapes=[
            pltpu.VMEM((rows, pieces[0].shape[1]), BF16),
            pltpu.VMEM(tables[0].shape, BF16),
            pltpu.SemaphoreType.DMA((-(-vocab // 512),)),
        ],
        compiler_params=pltpu.CompilerParams(vmem_limit_bytes=36 << 20),
        cost_estimate=pl.CostEstimate(
            flops=4 * rows * vocab * D,
            bytes_accessed=4 * vocab * D,
            transcendentals=4 * rows * vocab,
        ),
    )(bases, mark.reshape(rows, 1), tables[1], tables[0], *pieces)


def per_device(
    queries,
    new_keys,
    new_values,
    stored_keys,
    stored_values,
    lengths,
    out_proj,
    residual,
    norm_gain,
    embedding,
    targets,
    old_sums,
    rewards,
    group_ids,
):
    nx, ny, nz, nc = (lax.axis_size(a) for a in TP_REP)
    x, y, z, c = (lax.axis_index(a) for a in TP_REP)
    samp = queries.shape[0]
    cols = out_proj.shape[1]
    vocab = embedding.shape[0]
    reps = ny * nz * nc
    groups = samp * reps // GROUP
    per_x = nz // nx
    rows = per_x * samp
    width = nc * cols

    other_embedding = shifted(embedding, "c", 1)
    proj, res = out_proj.T, residual.T
    feats, window = proj.shape[1], 2 * rows * nc

    def with_residual(k):
        start = ((y - k) % ny) * (nx * rows * nc) + (x // 2) * window
        return jnp.concatenate([proj, lax.dynamic_slice_in_dim(res, start, window, 1)], 1)

    both = [with_residual(0)] + [shifted(with_residual(k), "y", k) for k in range(1, ny)]
    both = rolled(jnp.stack(both), (ny - y) % ny, 0)
    both_other = shifted(both, "c", 1)
    both = jnp.where(
        c == 0, jnp.stack([both, both_other], 1), jnp.stack([both_other, both], 1)
    ).reshape(ny * nc, cols, feats + window)
    proj, res = both[:, :, :feats].reshape(ny * width, feats), both[:, :, feats:]
    context = attention(
        queries, new_keys, new_values, stored_keys, stored_values, lengths, nz
    )
    context = lax.all_to_all(context, "z", 0, 0, tiled=True).reshape(nz * samp, -1)

    member = group_ids[:, None] == lax.broadcasted_iota(jnp.int32, (1, groups), 1)
    reward_part = jnp.sum(jnp.where(member, rewards[:, None], 0.0), 0)
    reward_part = reward_part + shifted(reward_part, "c", 1)

    partial = lax.dot_general(context, proj, NT, preferred_element_type=F32)
    partial = partial.reshape(nx, rows, ny * width)

    def quarter(k):
        return lax.dynamic_index_in_dim(partial, (x + k) % nx, 0, False)

    heads = [quarter(0)] + [shifted(quarter(k), "x", -k) for k in range(1, nx)]
    gain = lax.dynamic_index_in_dim(norm_gain.reshape(ny, nz, width), z, 1, False)
    stream = pl.pallas_call(
        functools.partial(stream_kernel, samp=samp),
        out_shape=jax.ShapeDtypeStruct((nz, rows, ny * width), BF16),
        in_specs=[SMEM] + [VMEM] * 6,
        out_specs=VMEM,
        compiler_params=pltpu.CompilerParams(vmem_limit_bytes=8 << 20),
        name="stream",
    )(jnp.stack([x % 2, c]), *heads, res, gain.reshape(1, ny * width))
    stream = lax.all_to_all(stream, "z", 0, 0, tiled=True)

    block = pl.pallas_call(
        functools.partial(assemble_kernel, ny=ny),
        out_shape=jax.ShapeDtypeStruct((rows, D + 128), BF16),
        in_specs=[VMEM] * 2,
        out_specs=VMEM,
        compiler_params=pltpu.CompilerParams(vmem_limit_bytes=16 << 20),
        name="assemble",
    )(stream, (1.0 / norm_gain)[None])

    first, second = block[:samp], block[samp:]
    row_x, row_y = [first], [second]
    for k in range(1, nx):
        row_x.append(shifted(first, "x", k))
        row_y.append(shifted(second, "y", k))
    row_x, row_y = jnp.concatenate(row_x), jnp.concatenate(row_y)
    x_far, y_far = {0: row_x}, {0: row_y}
    for k in (1, nx - 1, 2):
        x_far[k], y_far[k] = shifted(row_x, "y", k), shifted(row_y, "x", k)

    marks = targets.reshape(ny, nx, per_x, nc, samp)
    marks = lax.dynamic_index_in_dim(marks, c, 3, False)
    marks = rolled(rolled(marks, y, 0), x, 1)
    marks_x = marks[:, :, 0].reshape(ny, nx * samp)
    marks_y = marks[:, :, 1].swapaxes(0, 1).reshape(nx, ny * samp)
    shard = (x * reps + (y * nz + z) * nc) * vocab
    bases = jnp.stack([shard + c * vocab, shard + (1 - c) * vocab])

    size = nx * samp
    part = {}
    for of in ((0,), (1, 3), (2,)):
        mark = jnp.concatenate([marks_x[k] for k in of] + [marks_y[k] for k in of])
        pieces = [x_far[k] for k in of] + [y_far[k] for k in of]
        found = losses(pieces, mark, (embedding, other_embedding), bases)
        for i, key in enumerate([("x", k) for k in of] + [("y", k) for k in of]):
            part[key] = found[:2, i * size : (i + 1) * size]
    half_x = jnp.stack([part["x", k] for k in range(ny)], 1).reshape(2, ny, nx, samp)
    half_y = jnp.stack([part["y", k] for k in range(nx)], 1).reshape(2, nx, ny, samp)
    half_y = half_y.swapaxes(1, 2)
    both = jnp.stack([half_x, half_y], 3)
    both = rolled(rolled(both, (ny - y) % ny, 1), (nx - x) % nx, 2)
    both = both.transpose(1, 2, 3, 0, 4).reshape(ny * nz, 2 * samp)
    both = jnp.broadcast_to(both[None], (nx, *both.shape)).reshape(nx * ny * nz, 2 * samp)
    spread = jnp.broadcast_to(reward_part[None], (nx * ny * nz, groups))
    payload = jnp.concatenate([both, spread], 1)
    payload = jnp.pad(payload, ((0, 0), (0, 256 - payload.shape[1])))[:, None]
    got = lax.all_to_all(payload, ("x", "y", "z"), 0, 0, tiled=True)[:, 0]
    sums = jnp.sum(got[:, : 2 * samp], 0)
    logprob_sum = old_sums + (sums[samp:] - jnp.log(sums[:samp]))
    group_total = jnp.sum(got[: ny * nz, 2 * samp : 2 * samp + groups], 0)
    mine = jnp.sum(jnp.where(member, group_total[None, :], 0.0), 1)
    advantage = rewards - (mine - rewards) / (GROUP - 1.0)
    return (logprob_sum, advantage)


def solution(mesh):
    split = Mesh(mesh.devices.reshape(mesh.shape["tp"], 4, 8, 2), TP_REP)
    placed = (
        P(REP, "x"),
        P(REP, "x"),
        P(REP, "x"),
        P(REP, "x", None, None),
        P(REP, "x", None, None),
        P(REP),
        P("x", REP),
        P(None, REP),
        P(),
        P(TP_REP, None),
        P(),
        P(REP),
        P(REP),
        P(REP),
    )

    return jax.shard_map(
        per_device, mesh=split, in_specs=placed, out_specs=(P(REP), P(REP)), check_vma=False
    )
```

time: 237 us -> 169 us (0.71)
  the two profiles are of different devices: /device:TPU:1 before, /device:TPU:8 now
where the time goes in v1:
time: 169 us
  waiting for transfers between devices  58.8 us (35%)
  starting transfers between devices  40.8 us (24%)
  Pallas kernels  37.7 us (22%)
  blocking collectives  19 us (11%)
  local copies, waits for them, and re-layouts  6.98 us (4%)
  other arithmetic  3.88 us (2%)
    ppermute x21, waiting for transfers between devices, shifted(): return lax.ppermute(x, axis, [((i + offset) % n, i) for i in range(n)])  36.3 us
    pallas_call x3, Pallas kernels, losses(): pl.pallas_call(functools.partial(loss_kernel, blocks=len(pieces)), out_sh...  30.3 us
    ppermute x21, starting transfers between devices, shifted(): return lax.ppermute(x, axis, [((i + offset) % n, i) for i in range(n)])  28.9 us
    all_to_all x1, blocking collectives, per_device(): got = lax.all_to_all(payload, ('x', 'y', 'z'), 0, 0, tiled=True)[:, 0]  19 us
    all_to_all x1, waiting for transfers between devices, per_device(): lax.all_to_all(context, 'z', 0, 0, tiled=True).reshape(nz * samp, -1)  11.4 us
    all_to_all x1, waiting for transfers between devices, per_device(): stream = lax.all_to_all(stream, 'z', 0, 0, tiled=True)  11.2 us
    all_to_all x1, starting transfers between devices, per_device(): lax.all_to_all(context, 'z', 0, 0, tiled=True).reshape(nz * samp, -1)  8.48 us
    pallas_call x1, Pallas kernels, attention(): pl.pallas_call(attention_kernel, out_shape=jax.ShapeDtypeStruct((copies,...  5.6 us
  transfers between devices with their start and end apart: 23, of which 13 were waited for; matrix products, arithmetic and copies ran while one was open for 4% of the time, Pallas kernels for 10%

profile of v1, /device:TPU:8, one launch (start us, length us, event | category | flops | bytes accessed | tf_op | source)
XLA Modules:
  0.0 168.8 jit_solution(16456988981742626592)
XLA Ops:
  2.6 2.2 %collective-permute-start.1 = (bf16[72,1152]{1,0:T(8,128)(2,1)S(1)}, bf16[72,1152]{1,0:T(8,128)(2,1)S(1)}, u32[]{:S(2)}, u32[]{:S(2)}) collective-permute-start(bf16[72,1152]{1,0:T(8,128)(2,1)S(1)} %get-tuple-element.17), channel_id=1, source_target_pairs={{16,0},{32,16},{48,32},{0,48},{17,1},{33,17},{49,33},{1,49},{18,2}... | collective-permute-start | bytes 497672 | tf_op jit(solution)/shard_map/ppermute | solution.py:21
  5.7 1.9 %collective-permute-start.3 = (bf16[72,1152]{1,0:T(8,128)(2,1)S(1)}, bf16[72,1152]{1,0:T(8,128)(2,1)S(1)}, u32[]{:S(2)}, u32[]{:S(2)}) collective-permute-start(bf16[72,1152]{1,0:T(8,128)(2,1)S(1)} %get-tuple-element.16), channel_id=1, source_target_pairs={{48,0},{0,16},{16,32},{32,48},{49,1},{1,17},{17,33},{33,49},{50,2}... | collective-permute-start | bytes 497672 | tf_op jit(solution)/shard_map/ppermute | solution.py:21
  9.5 4.3 %collective-permute-done.2 = bf16[72,1152]{1,0:T(8,128)(2,1)S(1)} collective-permute-done((bf16[72,1152]{1,0:T(8,128)(2,1)S(1)}, bf16[72,1152]{1,0:T(8,128)(2,1)S(1)}, u32[]{:S(2)}, u32[]{:S(2)}) %collective-permute-start.2) | collective-permute-done | bytes 165920 | tf_op jit(solution)/shard_map/ppermute | solution.py:21
  15.9 5.6 %attend.1 = bf16[8,16,1024]{2,1,0:T(8,128)(2,1)} custom-call(s32[16,1]{1,0:T(8,128)} %copy.54.lengths_ref, bf16[16,1024]{1,0:T(8,128)(2,1)} %q_ref.1, bf16[16,512]{1,0:T(8,128)(2,1)} %nk_ref.1, bf16[16,512]{1,0:T(8,128)(2,1)} %nv_ref.1, bf16[16,4,128,128]{3,2,1,0:T(8,128)(2,1)} %k_hbm.1, bf16[16,4,128,128]{3,2,1,0:T(8,128)(2,1)} %v_hbm.1), custom_call_target="tpu_custom_call" | custom-call | flops 4294967296 | bytes 4194304 | tf_op jit(solution)/shard_map/attend/pallas_call | solution.py:81
  21.5 8.5 %all-to-all-start = ((bf16[8,16,1024]{2,1,0:T(8,128)(2,1)}), bf16[8,16,1024]{2,1,0:T(8,128)(2,1)S(1)}, u32[]{:S(2)}, u32[]{:S(2)}) async-start(bf16[8,16,1024]{2,1,0:T(8,128)(2,1)} %attend.1), calls=%async_computation | async-start | bytes 524288 | tf_op jit(solution)/shard_map/all_to_all | solution.py:234
  30.8 11.4 %all-to-all-done = bf16[8,16,1024]{2,1,0:T(8,128)(2,1)S(1)} async-done(((bf16[8,16,1024]{2,1,0:T(8,128)(2,1)}), bf16[8,16,1024]{2,1,0:T(8,128)(2,1)S(1)}, u32[]{:S(2)}, u32[]{:S(2)}) %all-to-all-start) | async-done | bytes 262176 | tf_op jit(solution)/shard_map/all_to_all | solution.py:234
  42.8 1.6 collective-permute-start.5
  44.3 2.7 %collective-permute-start.6 = (f32[32,576]{1,0:T(8,128)S(1)}, f32[32,576]{1,0:T(8,128)S(1)}, u32[]{:S(2)}, u32[]{:S(2)}) collective-permute-start(f32[32,576]{1,0:T(8,128)S(1)} %get-tuple-element.11), channel_id=1, source_target_pairs={{128,0},{192,64},{0,128},{64,192},{129,1},{193,65},{1,129},{65,193... | collective-permute-start | bytes 221192 | tf_op jit(solution)/shard_map/ppermute | solution.py:21
  47.1 1.4 collective-permute-start.7
  52.9 3.4 %all-to-all-start.1 = ((bf16[8,32,576]{2,1,0:T(8,128)(2,1)}), bf16[8,32,576]{2,1,0:T(8,128)(2,1)S(1)}, u32[]{:S(2)}, u32[]{:S(2)}) async-start(bf16[8,32,576]{2,1,0:T(8,128)(2,1)} %stream.1), calls=%async_computation.1 | async-start | bytes 655360 | tf_op jit(solution)/shard_map/all_to_all | solution.py:256
  56.4 11.2 %all-to-all-done.1.got_ref = bf16[8,32,576]{2,1,0:T(8,128)(2,1)S(1)} async-done(((bf16[8,32,576]{2,1,0:T(8,128)(2,1)}), bf16[8,32,576]{2,1,0:T(8,128)(2,1)S(1)}, u32[]{:S(2)}, u32[]{:S(2)}) %all-to-all-start.1) | async-done | bytes 294944 | tf_op jit(solution)/shard_map/all_to_all | solution.py:256
  67.9 3.0 %collective-permute-start.11 = (bf16[16,4736]{1,0:T(8,128)(2,1)S(1)}, bf16[16,4736]{1,0:T(8,128)(2,1)S(1)}, u32[]{:S(2)}, u32[]{:S(2)}) collective-permute-start(bf16[16,4736]{1,0:T(8,128)(2,1)S(1)} %get-tuple-element.14), channel_id=1, source_target_pairs={{16,0},{32,16},{48,32},{0,48},{17,1},{33,17},{49,33},{1,49},{18,2}... | collective-permute-start | bytes 454664 | tf_op jit(solution)/shard_map/ppermute | solution.py:21
  70.9 2.0 %collective-permute-start.13 = (bf16[16,4736]{1,0:T(8,128)(2,1)S(1)}, bf16[16,4736]{1,0:T(8,128)(2,1)S(1)}, u32[]{:S(2)}, u32[]{:S(2)}) collective-permute-start(bf16[16,4736]{1,0:T(8,128)(2,1)S(1)} %get-tuple-element.14), channel_id=1, source_target_pairs={{48,0},{0,16},{16,32},{32,48},{49,1},{1,17},{17,33},{33,49},{50,2}... | collective-permute-start | bytes 454664 | tf_op jit(solution)/shard_map/ppermute | solution.py:21
  74.8 2.8 %collective-permute-done.12 = bf16[16,4736]{1,0:T(8,128)(2,1)S(1)} collective-permute-done((bf16[16,4736]{1,0:T(8,128)(2,1)S(1)}, bf16[16,4736]{1,0:T(8,128)(2,1)S(1)}, u32[]{:S(2)}, u32[]{:S(2)}) %collective-permute-start.12) | collective-permute-done | bytes 151584 | tf_op jit(solution)/shard_map/ppermute | solution.py:21
  77.6 2.6 %collective-permute-start.8 = (bf16[16,4736]{1,0:T(8,128)(2,1)S(1)}, bf16[16,4736]{1,0:T(8,128)(2,1)S(1)}, u32[]{:S(2)}, u32[]{:S(2)}) collective-permute-start(bf16[16,4736]{1,0:T(8,128)(2,1)S(1)} %get-tuple-element.15), channel_id=1, source_target_pairs={{64,0},{128,64},{192,128},{0,192},{65,1},{129,65},{193,129},{1,193... | collective-permute-start | bytes 454664 | tf_op jit(solution)/shard_map/ppermute | solution.py:21
  81.4 2.5 %collective-permute-start.19 = (bf16[64,4736]{1,0:T(8,128)(2,1)S(1)}, bf16[64,4736]{1,0:T(8,128)(2,1)S(1)}, u32[]{:S(2)}, u32[]{:S(2)}) collective-permute-start(bf16[64,4736]{1,0:T(8,128)(2,1)S(1)} %pad_maximum_fusion.1.refs_5_), channel_id=1, source_target_pairs={{128,0},{192,64},{0,128},{64,192},{129,1},{193,65},{1,129},{65,193... | collective-permute-start | bytes 1818632 | tf_op jit(solution)/shard_map/ppermute | solution.py:21
  83.9 14.3 %collective-permute-done.8 = bf16[16,4736]{1,0:T(8,128)(2,1)S(1)} collective-permute-done((bf16[16,4736]{1,0:T(8,128)(2,1)S(1)}, bf16[16,4736]{1,0:T(8,128)(2,1)S(1)}, u32[]{:S(2)}, u32[]{:S(2)}) %collective-permute-start.8) | collective-permute-done | bytes 151584 | tf_op jit(solution)/shard_map/ppermute | solution.py:21
  100.4 4.2 %collective-permute-start.16 = (bf16[64,4736]{1,0:T(8,128)(2,1)S(1)}, bf16[64,4736]{1,0:T(8,128)(2,1)S(1)}, u32[]{:S(2)}, u32[]{:S(2)}) collective-permute-start(bf16[64,4736]{1,0:T(8,128)(2,1)S(1)} %pad_maximum_fusion.1.refs_5_), channel_id=1, source_target_pairs={{64,0},{128,64},{192,128},{0,192},{65,1},{129,65},{193,129},{1,193... | collective-permute-start | bytes 1818632 | tf_op jit(solution)/shard_map/ppermute | solution.py:21
  105.5 2.0 %collective-permute-start.14 = (bf16[64,4736]{1,0:T(8,128)(2,1)S(1)}, bf16[64,4736]{1,0:T(8,128)(2,1)S(1)}, u32[]{:S(2)}, u32[]{:S(2)}) collective-permute-start(bf16[64,4736]{1,0:T(8,128)(2,1)S(1)} %pad_maximum_fusion.refs_4_), channel_id=1, source_target_pairs={{16,0},{32,16},{48,32},{0,48},{17,1},{33,17},{49,33},{1,49},{18,2}... | collective-permute-start | bytes 1818632 | tf_op jit(solution)/shard_map/ppermute | solution.py:21
  107.5 8.0 %collective-permute-done.18.refs_4_ = bf16[64,4736]{1,0:T(8,128)(2,1)} collective-permute-done((bf16[64,4736]{1,0:T(8,128)(2,1)S(1)}, bf16[64,4736]{1,0:T(8,128)(2,1)}, u32[]{:S(2)}, u32[]{:S(2)}) %collective-permute-start.18) | collective-permute-done | bytes 606240 | tf_op jit(solution)/shard_map/ppermute | solution.py:21
  117.2 10.3 %shard_map.151 = f32[8,128]{1,0:T(8,128)S(1)} custom-call(s32[2]{0:T(128)S(1)} %pad_add_fusion.1.refs_0_, s32[128,1]{1,0:T(8,128)S(1)} %copy.58.refs_1_, bf16[1000,4608]{1,0:T(8,128)(2,1)} %collective-permute-done.refs_2_, bf16[1000,4608]{1,0:T(8,128)(2,1)} %refs_3_.5, bf16[64,4736]{1,0:T(8,128)(2,1)} %collective-permute-done.18.refs_4_, ...), custom_call_target="tpu_custom_call" | custom-call | flops 2359296000 | bytes 18432000 | tf_op jit(solution)/shard_map/pallas_call | solution.py:170
  127.7 9.8 %shard_map.150 = f32[8,256]{1,0:T(8,128)S(1)} custom-call(s32[2]{0:T(128)S(1)} %pad_add_fusion.1.refs_0_, s32[256,1]{1,0:T(8,128)S(1)} %copy.57.refs_1_, bf16[1000,4608]{1,0:T(8,128)(2,1)} %collective-permute-done.refs_2_, bf16[1000,4608]{1,0:T(8,128)(2,1)} %refs_3_.5, bf16[64,4736]{1,0:T(8,128)(2,1)S(1)} %collective-permute-done.14.refs_4_, ...), custom_call_target="tpu_custom_call" | custom-call | flops 4718592000 | bytes 18432000 | tf_op jit(solution)/shard_map/pallas_call | solution.py:170
  137.8 10.2 %shard_map.149 = f32[8,128]{1,0:T(8,128)S(1)} custom-call(s32[2]{0:T(128)S(1)} %pad_add_fusion.1.refs_0_, s32[128,1]{1,0:T(8,128)S(1)} %copy.56.refs_1_, bf16[1000,4608]{1,0:T(8,128)(2,1)} %collective-permute-done.refs_2_, bf16[1000,4608]{1,0:T(8,128)(2,1)} %refs_3_.5, bf16[64,4736]{1,0:T(8,128)(2,1)S(1)} %pad_maximum_fusion.refs_4_, ...), custom_call_target="tpu_custom_call" | custom-call | flops 2359296000 | bytes 18432000 | tf_op jit(solution)/shard_map/pallas_call | solution.py:170
  148.9 19.0 %all_to_all.15 = f32[128,1,256]{2,1,0:T(1,128)S(1)} all-to-all(f32[128,1,256]{2,1,0:T(1,128)S(1)} %broadcast_in_dim.50), channel_id=1, replica_groups=mesh['x'=4,'y'=4,'z'=8,'c'=2] {'x','y','z'}, dimensions={0} | all-to-all | bytes 262144 | tf_op jit(solution)/shard_map/all_to_all | solution.py:303
  (129 shorter events, 22.7 us)
Async XLA Ops:
  0.6 115.4 %collective-permute-start = (bf16[1000,4608]{1,0:T(8,128)(2,1)}, bf16[1000,4608]{1,0:T(8,128)(2,1)}, u32[]{:S(2)}, u32[]{:S(2)}) collective-permute-start(bf16[1000,4608]{1,0:T(8,128)(2,1)} %refs_3_.5), channel_id=1, source_target_pairs={{1,0},{0,1},{3,2},{2,3},{5,4},{4,5},{7,6},{6,7},{9,8},{8,9},{11,10... | collective-permute-start | bytes 27648008 | tf_op jit(solution)/shard_map/ppermute | solution.py:21
  2.6 6.9 %collective-permute-start.1 = (bf16[72,1152]{1,0:T(8,128)(2,1)S(1)}, bf16[72,1152]{1,0:T(8,128)(2,1)S(1)}, u32[]{:S(2)}, u32[]{:S(2)}) collective-permute-start(bf16[72,1152]{1,0:T(8,128)(2,1)S(1)} %get-tuple-element.17), channel_id=1, source_target_pairs={{16,0},{32,16},{48,32},{0,48},{17,1},{33,17},{49,33},{1,49},{18,2}... | collective-permute-start | bytes 497672 | tf_op jit(solution)/shard_map/ppermute | solution.py:21
  4.8 8.9 %collective-permute-start.2 = (bf16[72,1152]{1,0:T(8,128)(2,1)S(1)}, bf16[72,1152]{1,0:T(8,128)(2,1)S(1)}, u32[]{:S(2)}, u32[]{:S(2)}) collective-permute-start(bf16[72,1152]{1,0:T(8,128)(2,1)S(1)} %get-tuple-element.18), channel_id=1, source_target_pairs={{32,0},{48,16},{0,32},{16,48},{33,1},{49,17},{1,33},{17,49},{34,2}... | collective-permute-start | bytes 497672 | tf_op jit(solution)/shard_map/ppermute | solution.py:21
  5.7 8.9 %collective-permute-start.3 = (bf16[72,1152]{1,0:T(8,128)(2,1)S(1)}, bf16[72,1152]{1,0:T(8,128)(2,1)S(1)}, u32[]{:S(2)}, u32[]{:S(2)}) collective-permute-start(bf16[72,1152]{1,0:T(8,128)(2,1)S(1)} %get-tuple-element.16), channel_id=1, source_target_pairs={{48,0},{0,16},{16,32},{32,48},{49,1},{1,17},{17,33},{33,49},{50,2}... | collective-permute-start | bytes 497672 | tf_op jit(solution)/shard_map/ppermute | solution.py:21
  14.8 15.5 %collective-permute-start.4 = (bf16[4,72,1152]{2,1,0:T(8,128)(2,1)S(1)}, bf16[4,72,1152]{2,1,0:T(8,128)(2,1)S(1)}, u32[]{:S(2)}, u32[]{:S(2)}) collective-permute-start(bf16[4,72,1152]{2,1,0:T(8,128)(2,1)S(1)} %constant_dynamic-slice_fusion.1), channel_id=1, source_target_pairs={{1,0},{0,1},{3,2},{2,3},{5,4},{4,5},{7,6},{6,7},{9,8},{8,9},{11,10... | collective-permute-start | bytes 1990664 | tf_op jit(solution)/shard_map/ppermute | solution.py:21
  21.5 20.6 %all-to-all-start = ((bf16[8,16,1024]{2,1,0:T(8,128)(2,1)}), bf16[8,16,1024]{2,1,0:T(8,128)(2,1)S(1)}, u32[]{:S(2)}, u32[]{:S(2)}) async-start(bf16[8,16,1024]{2,1,0:T(8,128)(2,1)} %attend.1), calls=%async_computation | async-start | bytes 524288 | tf_op jit(solution)/shard_map/all_to_all | solution.py:234
  42.8 6.3 %collective-permute-start.5 = (f32[32,576]{1,0:T(8,128)S(1)}, f32[32,576]{1,0:T(8,128)S(1)}, u32[]{:S(2)}, u32[]{:S(2)}) collective-permute-start(f32[32,576]{1,0:T(8,128)S(1)} %get-tuple-element.12), channel_id=1, source_target_pairs={{192,0},{0,64},{64,128},{128,192},{193,1},{1,65},{65,129},{129,193... | collective-permute-start | bytes 221192 | tf_op jit(solution)/shard_map/ppermute | solution.py:21
  44.3 6.0 %collective-permute-start.6 = (f32[32,576]{1,0:T(8,128)S(1)}, f32[32,576]{1,0:T(8,128)S(1)}, u32[]{:S(2)}, u32[]{:S(2)}) collective-permute-start(f32[32,576]{1,0:T(8,128)S(1)} %get-tuple-element.11), channel_id=1, source_target_pairs={{128,0},{192,64},{0,128},{64,192},{129,1},{193,65},{1,129},{65,193... | collective-permute-start | bytes 221192 | tf_op jit(solution)/shard_map/ppermute | solution.py:21
  47.1 4.4 %collective-permute-start.7 = (f32[32,576]{1,0:T(8,128)S(1)}, f32[32,576]{1,0:T(8,128)S(1)}, u32[]{:S(2)}, u32[]{:S(2)}) collective-permute-start(f32[32,576]{1,0:T(8,128)S(1)} %get-tuple-element.10), channel_id=1, source_target_pairs={{64,0},{128,64},{192,128},{0,192},{65,1},{129,65},{193,129},{1,193... | collective-permute-start | bytes 221192 | tf_op jit(solution)/shard_map/ppermute | solution.py:21
  51.5 21.6 %copy-start.4 = (s32[1024]{0:T(1024)S(1)}, s32[1024]{0:T(1024)}, u32[]{:S(2)}) copy-start(s32[1024]{0:T(1024)} %param.24) | copy-start | bytes 12292
  52.9 14.7 %all-to-all-start.1 = ((bf16[8,32,576]{2,1,0:T(8,128)(2,1)}), bf16[8,32,576]{2,1,0:T(8,128)(2,1)S(1)}, u32[]{:S(2)}, u32[]{:S(2)}) async-start(bf16[8,32,576]{2,1,0:T(8,128)(2,1)} %stream.1), calls=%async_computation.1 | async-start | bytes 655360 | tf_op jit(solution)/shard_map/all_to_all | solution.py:256
  67.9 6.5 %collective-permute-start.11 = (bf16[16,4736]{1,0:T(8,128)(2,1)S(1)}, bf16[16,4736]{1,0:T(8,128)(2,1)S(1)}, u32[]{:S(2)}, u32[]{:S(2)}) collective-permute-start(bf16[16,4736]{1,0:T(8,128)(2,1)S(1)} %get-tuple-element.14), channel_id=1, source_target_pairs={{16,0},{32,16},{48,32},{0,48},{17,1},{33,17},{49,33},{1,49},{18,2}... | collective-permute-start | bytes 454664 | tf_op jit(solution)/shard_map/ppermute | solution.py:21
  70.9 6.7 %collective-permute-start.12 = (bf16[16,4736]{1,0:T(8,128)(2,1)S(1)}, bf16[16,4736]{1,0:T(8,128)(2,1)S(1)}, u32[]{:S(2)}, u32[]{:S(2)}) collective-permute-start(bf16[16,4736]{1,0:T(8,128)(2,1)S(1)} %get-tuple-element.14), channel_id=1, source_target_pairs={{32,0},{48,16},{0,32},{16,48},{33,1},{49,17},{1,33},{17,49},{34,2}... | collective-permute-start | bytes 454664 | tf_op jit(solution)/shard_map/ppermute | solution.py:21
  70.9 9.3 %collective-permute-start.13 = (bf16[16,4736]{1,0:T(8,128)(2,1)S(1)}, bf16[16,4736]{1,0:T(8,128)(2,1)S(1)}, u32[]{:S(2)}, u32[]{:S(2)}) collective-permute-start(bf16[16,4736]{1,0:T(8,128)(2,1)S(1)} %get-tuple-element.14), channel_id=1, source_target_pairs={{48,0},{0,16},{16,32},{32,48},{49,1},{1,17},{17,33},{33,49},{50,2}... | collective-permute-start | bytes 454664 | tf_op jit(solution)/shard_map/ppermute | solution.py:21
  73.1 31.6 %collective-permute-start.20 = (f32[128]{0:T(128)S(1)}, f32[128]{0:T(128)S(1)}, u32[]{:S(2)}, u32[]{:S(2)}) collective-permute-start(f32[128]{0:T(128)S(1)} %select_reduce_fusion.1), channel_id=1, source_target_pairs={{1,0},{0,1},{3,2},{2,3},{5,4},{4,5},{7,6},{6,7},{9,8},{8,9},{11,10... | collective-permute-start | bytes 1544 | tf_op jit(solution)/shard_map/ppermute | solution.py:21
  74.5 6.9 %collective-permute-start.10 = (bf16[16,4736]{1,0:T(8,128)(2,1)S(1)}, bf16[16,4736]{1,0:T(8,128)(2,1)S(1)}, u32[]{:S(2)}, u32[]{:S(2)}) collective-permute-start(bf16[16,4736]{1,0:T(8,128)(2,1)S(1)} %get-tuple-element.15), channel_id=1, source_target_pairs={{192,0},{0,64},{64,128},{128,192},{193,1},{1,65},{65,129},{129,193... | collective-permute-start | bytes 454664 | tf_op jit(solution)/shard_map/ppermute | solution.py:21
  77.6 20.6 %collective-permute-start.8 = (bf16[16,4736]{1,0:T(8,128)(2,1)S(1)}, bf16[16,4736]{1,0:T(8,128)(2,1)S(1)}, u32[]{:S(2)}, u32[]{:S(2)}) collective-permute-start(bf16[16,4736]{1,0:T(8,128)(2,1)S(1)} %get-tuple-element.15), channel_id=1, source_target_pairs={{64,0},{128,64},{192,128},{0,192},{65,1},{129,65},{193,129},{1,193... | collective-permute-start | bytes 454664 | tf_op jit(solution)/shard_map/ppermute | solution.py:21
  80.2 18.0 %collective-permute-start.9 = (bf16[16,4736]{1,0:T(8,128)(2,1)S(1)}, bf16[16,4736]{1,0:T(8,128)(2,1)S(1)}, u32[]{:S(2)}, u32[]{:S(2)}) collective-permute-start(bf16[16,4736]{1,0:T(8,128)(2,1)S(1)} %get-tuple-element.15), channel_id=1, source_target_pairs={{128,0},{192,64},{0,128},{64,192},{129,1},{193,65},{1,129},{65,193... | collective-permute-start | bytes 454664 | tf_op jit(solution)/shard_map/ppermute | solution.py:21
  81.4 23.3 %collective-permute-start.19 = (bf16[64,4736]{1,0:T(8,128)(2,1)S(1)}, bf16[64,4736]{1,0:T(8,128)(2,1)S(1)}, u32[]{:S(2)}, u32[]{:S(2)}) collective-permute-start(bf16[64,4736]{1,0:T(8,128)(2,1)S(1)} %pad_maximum_fusion.1.refs_5_), channel_id=1, source_target_pairs={{128,0},{192,64},{0,128},{64,192},{129,1},{193,65},{1,129},{65,193... | collective-permute-start | bytes 1818632 | tf_op jit(solution)/shard_map/ppermute | solution.py:21
  98.3 17.2 %collective-permute-start.18 = (bf16[64,4736]{1,0:T(8,128)(2,1)S(1)}, bf16[64,4736]{1,0:T(8,128)(2,1)}, u32[]{:S(2)}, u32[]{:S(2)}) collective-permute-start(bf16[64,4736]{1,0:T(8,128)(2,1)S(1)} %pad_maximum_fusion.refs_4_), channel_id=1, source_target_pairs={{32,0},{48,16},{0,32},{16,48},{33,1},{49,17},{1,33},{17,49},{34,2}... | collective-permute-start | bytes 1818632 | tf_op jit(solution)/shard_map/ppermute | solution.py:21
  100.4 27.2 %collective-permute-start.16 = (bf16[64,4736]{1,0:T(8,128)(2,1)S(1)}, bf16[64,4736]{1,0:T(8,128)(2,1)S(1)}, u32[]{:S(2)}, u32[]{:S(2)}) collective-permute-start(bf16[64,4736]{1,0:T(8,128)(2,1)S(1)} %pad_maximum_fusion.1.refs_5_), channel_id=1, source_target_pairs={{64,0},{128,64},{192,128},{0,192},{65,1},{129,65},{193,129},{1,193... | collective-permute-start | bytes 1818632 | tf_op jit(solution)/shard_map/ppermute | solution.py:21
  104.6 23.0 %collective-permute-start.17 = (bf16[64,4736]{1,0:T(8,128)(2,1)S(1)}, bf16[64,4736]{1,0:T(8,128)(2,1)S(1)}, u32[]{:S(2)}, u32[]{:S(2)}) collective-permute-start(bf16[64,4736]{1,0:T(8,128)(2,1)S(1)} %pad_maximum_fusion.1.refs_5_), channel_id=1, source_target_pairs={{192,0},{0,64},{64,128},{128,192},{193,1},{1,65},{65,129},{129,193... | collective-permute-start | bytes 1818632 | tf_op jit(solution)/shard_map/ppermute | solution.py:21
  105.5 22.2 %collective-permute-start.14 = (bf16[64,4736]{1,0:T(8,128)(2,1)S(1)}, bf16[64,4736]{1,0:T(8,128)(2,1)S(1)}, u32[]{:S(2)}, u32[]{:S(2)}) collective-permute-start(bf16[64,4736]{1,0:T(8,128)(2,1)S(1)} %pad_maximum_fusion.refs_4_), channel_id=1, source_target_pairs={{16,0},{32,16},{48,32},{0,48},{17,1},{33,17},{49,33},{1,49},{18,2}... | collective-permute-start | bytes 1818632 | tf_op jit(solution)/shard_map/ppermute | solution.py:21
  115.5 12.2 %collective-permute-start.15 = (bf16[64,4736]{1,0:T(8,128)(2,1)S(1)}, bf16[64,4736]{1,0:T(8,128)(2,1)}, u32[]{:S(2)}, u32[]{:S(2)}) collective-permute-start(bf16[64,4736]{1,0:T(8,128)(2,1)S(1)} %pad_maximum_fusion.refs_4_), channel_id=1, source_target_pairs={{48,0},{0,16},{16,32},{32,48},{49,1},{1,17},{17,33},{33,49},{50,2}... | collective-permute-start | bytes 1818632 | tf_op jit(solution)/shard_map/ppermute | solution.py:21
  (8 other events, 93.8 us)

commit v2 on v1

--- a/solution.py
+++ b/solution.py
@@ -38,41 +38,49 @@
     copies, ratio = out_ref.shape[0], q_ref.shape[1] // (kv * depth)
     k_copy = [pltpu.make_async_copy(k_hbm.at[:, g], k_ref.at[g], k_sem.at[g]) for g in range(kv)]
     v_copy = [pltpu.make_async_copy(v_hbm.at[:, g], v_ref.at[g], v_sem.at[g]) for g in range(kv)]
-    for g in range(kv):
-        k_copy[g].start()
-        v_copy[g].start()
+    for copy in k_copy + v_copy:
+        copy.start()
     row = lax.broadcasted_iota(jnp.int32, (ratio * samp, span), 0)
-    slot = lax.broadcasted_iota(jnp.int32, (ratio * samp, span), 1)
     sample = lax.rem(row, samp)
-    live = jnp.concatenate([lengths_ref[...]] * ratio, 0)
-    for g in range(kv):
-        heads = [pl.ds((g * ratio + r) * depth, depth) for r in range(ratio)]
-        q = jnp.concatenate([q_ref[:, h].astype(F32) for h in heads], 0)
-        q16 = q.astype(BF16)
-        nk = jnp.concatenate([nk_ref[:, pl.ds(g * depth, depth)].astype(F32)] * ratio, 0)
-        nv = jnp.concatenate([nv_ref[:, pl.ds(g * depth, depth)].astype(F32)] * ratio, 0)
+    live = jnp.zeros((ratio * samp, span), jnp.int32)
+    for s in range(samp):
+        live = jnp.where(sample == s, lengths_ref[s], live)
+    live = lax.broadcasted_iota(jnp.int32, live.shape, 1) < live
+    heads = [[pl.ds((g * ratio + r) * depth, depth) for r in range(ratio)] for g in range(kv)]
+    queries = [jnp.concatenate([q_ref[:, h].astype(F32) for h in heads[g]], 0) for g in range(kv)]
+
+    def repeated(ref, g):
+        return jnp.concatenate([ref[:, pl.ds(g * depth, depth)].astype(F32)] * ratio, 0)
+
+    probs, own_probs = [], []
+    for g in range(kv):
+        own = jnp.sum(queries[g] * repeated(nk_ref, g), 1, keepdims=True)
+        own_probs.append(jnp.exp(50.0 * jnp.tanh(own / 12.0 / 50.0)))
+    for g in range(kv):
         k_copy[g].wait()
-        scores = jnp.zeros((ratio * samp, span), F32)
+    for g in range(kv):
+        q = queries[g].astype(BF16)
+        scores = jnp.zeros(live.shape, F32)
         for s in range(samp):
-            found = lax.dot_general(q16, k_ref[g, s], NT, preferred_element_type=F32)
+            found = lax.dot_general(q, k_ref[g, s], NT, preferred_element_type=F32)
             scores = jnp.where(sample == s, found, scores)
-        scores = 50.0 * jnp.tanh(scores / 12.0 / 50.0)
-        expo = jnp.where(slot < live, jnp.exp(scores), 0.0)
-        own = jnp.sum(q * nk, 1, keepdims=True)
-        own = jnp.exp(50.0 * jnp.tanh(own / 12.0 / 50.0))
-        total = jnp.sum(expo, 1, keepdims=True) + own
-        probs = (expo / total).astype(BF16)
-        own_prob = (own / total).astype(BF16).astype(F32)
+        probs.append(scores)
+    for g in range(kv):
+        expo = jnp.where(live, jnp.exp(50.0 * jnp.tanh(probs[g] / 12.0 / 50.0)), 0.0)
+        total = jnp.sum(expo, 1, keepdims=True) + own_probs[g]
+        probs[g] = (expo / total).astype(BF16)
+        own_probs[g] = (own_probs[g] / total).astype(BF16).astype(F32)
+    for g in range(kv):
         v_copy[g].wait()
-        out = own_prob * nv
-        found = jnp.zeros_like(out)
+    for g in range(kv):
+        found = jnp.zeros((ratio * samp, depth), F32)
         for s in range(samp):
-            one = jnp.dot(probs, v_ref[g, s], preferred_element_type=F32)
+            one = jnp.dot(probs[g], v_ref[g, s], preferred_element_type=F32)
             found = jnp.where(sample == s, one, found)
-        out = (found + out).astype(BF16)
+        out = (found + own_probs[g] * repeated(nv_ref, g)).astype(BF16)
         for r in range(ratio):
             for i in range(copies):
-                out_ref[i, :, heads[r]] = out[r * samp : (r + 1) * samp]
+                out_ref[i, :, heads[g][r]] = out[r * samp : (r + 1) * samp]
 
 
 def attention(queries, new_keys, new_values, stored_keys, stored_values, lengths, copies):
@@ -81,7 +89,7 @@
     return pl.pallas_call(
         attention_kernel,
         out_shape=jax.ShapeDtypeStruct((copies, *queries.shape), BF16),
-        in_specs=[VMEM, VMEM, VMEM, VMEM, hbm, hbm],
+        in_specs=[SMEM, VMEM, VMEM, VMEM, hbm, hbm],
         out_specs=VMEM,
         scratch_shapes=[
             pltpu.VMEM((kv, samp, span, depth), BF16),
@@ -94,7 +102,7 @@
             flops=4 << 30, bytes_accessed=4 << 20, transcendentals=1 << 16
         ),
         name="attend",
-    )(lengths.reshape(samp, 1), queries, new_keys, new_values, stored_keys, stored_values)
+    )(lengths, queries, new_keys, new_values, stored_keys, stored_values)
 
 
 def stream_kernel(at_ref, a_ref, b_ref, c_ref, d_ref, res_ref, gain_ref, out_ref, *, samp):
@@ -130,16 +138,20 @@
     out_ref[:, D:] = tail.astype(BF16)
 
 
-def loss_kernel(*refs, blocks):
+def windows(vocab, size):
+    starts = [min(at, vocab - size) for at in range(0, vocab, size)]
+    return [(lo, at - lo) for lo, at in zip(starts, range(0, vocab, size))]
+
+
+def loss_kernel(*refs, blocks, wide):
     base_ref, mark_ref, ready_ref, table_hbm = refs[:4]
     pieces = refs[4 : 4 + blocks]
     out_ref, rows_ref, table_ref, sem = refs[4 + blocks :]
     vocab = table_ref.shape[0]
-    cuts = [*range(0, vocab, 512), vocab]
-    parts = list(zip(cuts[:-1], cuts[1:]))
+    parts = windows(vocab, wide)
     copies = []
-    for i, (lo, hi) in enumerate(parts):
-        part = pl.ds(lo, hi - lo)
+    for i, (lo, seen) in enumerate(parts):
+        part = pl.ds(lo + seen, wide - seen)
         copies.append(pltpu.make_async_copy(table_hbm.at[part], table_ref.at[part], sem.at[i]))
         copies[i].start()
     rows = 0
@@ -147,19 +159,31 @@
         rows_ref[rows : rows + piece.shape[0]] = piece[...]
         rows += piece.shape[0]
     scale = jnp.sum(rows_ref[:, D:].astype(F32), 1, keepdims=True)
-    mark = mark_ref[...]
-    total = jnp.zeros((rows, 1), F32)
-    picked = jnp.zeros((rows, 1), F32)
+    lane = lax.broadcasted_iota(jnp.int32, (1, 128), 1)
+    mark = mark_ref[...] - lane
+    total = jnp.zeros((rows, 128), F32)
+    picked = jnp.zeros((rows, 128), F32)
     for which, ref in enumerate((ready_ref, table_ref)):
-        for i, (lo, hi) in enumerate(parts):
+        for i, (lo, seen) in enumerate(parts):
             if which:
                 copies[i].wait()
-            acc = lax.dot_general(rows_ref[:, :D], ref[lo:hi], NT, preferred_element_type=F32)
-            logits = 30.0 * jnp.tanh(acc * scale)
-            ids = base_ref[1 - which] + lo + lax.broadcasted_iota(jnp.int32, (1, hi - lo), 1)
-            total += jnp.sum(jnp.exp(logits), 1, keepdims=True)
-            picked += jnp.sum(jnp.where(ids == mark, logits, 0.0), 1, keepdims=True)
-    lane = lax.broadcasted_iota(jnp.int32, (rows, 128), 1)
+            acc = lax.dot_general(
+                rows_ref[:, :D], ref[lo : lo + wide], NT, preferred_element_type=F32
+            )
+            for at in range(0, wide, 128):
+                if seen >= at + 128:
+                    continue
+                soft = jnp.tanh(acc[:, at : at + 128] * scale)
+                expo = jnp.exp(30.0 * soft)
+                found = jnp.where(mark == base_ref[1 - which] + (lo + at), soft, 0.0)
+                if seen > at:
+                    fresh = lane >= seen - at
+                    expo = jnp.where(fresh, expo, 0.0)
+                    found = jnp.where(fresh, found, 0.0)
+                total += expo
+                picked += found
+    total = jnp.sum(total, 1, keepdims=True)
+    picked = jnp.sum(picked, 1, keepdims=True) * 30.0
     both = jnp.where(lane == 0, total, jnp.where(lane == 1, picked, 0.0))
     out_ref[...] = both.T[:8]
 
@@ -168,7 +192,7 @@
     rows = sum(p.shape[0] for p in pieces)
     vocab = tables[0].shape[0]
     return pl.pallas_call(
-        functools.partial(loss_kernel, blocks=len(pieces)),
+        functools.partial(loss_kernel, blocks=len(pieces), wide=512),
         out_shape=jax.ShapeDtypeStruct((8, rows), F32),
         in_specs=[SMEM, VMEM, VMEM, pl.BlockSpec(memory_space=pltpu.HBM)] + [VMEM] * len(pieces),
         out_specs=VMEM,
@@ -214,6 +238,10 @@
     width = nc * cols
 
     other_embedding = shifted(embedding, "c", 1)
+    context = attention(
+        queries, new_keys, new_values, stored_keys, stored_values, lengths, nz
+    )
+    out_proj, residual, context = lax.optimization_barrier((out_proj, residual, context))
     proj, res = out_proj.T, residual.T
     feats, window = proj.shape[1], 2 * rows * nc
 
@@ -228,9 +256,7 @@
         c == 0, jnp.stack([both, both_other], 1), jnp.stack([both_other, both], 1)
     ).reshape(ny * nc, cols, feats + window)
     proj, res = both[:, :, :feats].reshape(ny * width, feats), both[:, :, feats:]
-    context = attention(
-        queries, new_keys, new_values, stored_keys, stored_values, lengths, nz
-    )
+
     context = lax.all_to_all(context, "z", 0, 0, tiled=True).reshape(nz * samp, -1)
 
     member = group_ids[:, None] == lax.broadcasted_iota(jnp.int32, (1, groups), 1)
@@ -284,7 +310,7 @@
 
     size = nx * samp
     part = {}
-    for of in ((0,), (1, 3), (2,)):
+    for of in ((0,), (1, nx - 1, 2)):
         mark = jnp.concatenate([marks_x[k] for k in of] + [marks_y[k] for k in of])
         pieces = [x_far[k] for k in of] + [y_far[k] for k in of]
         found = losses(pieces, mark, (embedding, other_embedding), bases)

time: 169 us -> 160 us (0.947)
  starting transfers between devices: 40.8 us -> 49.2 us
  waiting for transfers between devices: 58.8 us -> 51.1 us
  Pallas kernels: 37.7 us -> 30.4 us
  local copies, waits for them, and re-layouts: 6.98 us -> 3.15 us
  blocking collectives: 19 us -> 20.7 us
    ppermute x21, waiting for transfers between devices: 36.3 us -> 27.2 us  [shifted(): return lax.ppermute(x, axis, [((i + offset) % n, i) for i in range(n)])]
    ppermute x21, starting transfers between devices: 28.9 us -> 37.3 us  [shifted(): return lax.ppermute(x, axis, [((i + offset) % n, i) for i in range(n)])]
    pallas_call x3 -> x2, Pallas kernels: 30.3 us -> 23 us  [losses(): pl.pallas_call(functools.partial(loss_kernel, blocks=len(pieces), wide=51...]
    unnamed x24 -> x20, local copies, waits for them, and re-layouts: 2.43 us -> 0.14 us
    all_to_all x1, blocking collectives: 19 us -> 20.7 us  [per_device(): got = lax.all_to_all(payload, ('x', 'y', 'z'), 0, 0, tiled=True)[:, 0]]
  transfers between devices with their start and end apart: 23 -> 23, of which waited for: 13 -> 12; matrix products, arithmetic and copies ran while one was open for 4% -> 3% of each run, Pallas kernels for 10% -> 11%
where the time goes in v2:
time: 160 us; the launch traced here: 159 us
  waiting for transfers between devices  51.1 us (32%)
  starting transfers between devices  49.2 us (31%)
  Pallas kernels  30.4 us (19%)
  blocking collectives  20.7 us (13%)
  local copies, waits for them, and re-layouts  3.15 us (2%)
  other arithmetic  2.84 us (2%)
    ppermute x21, starting transfers between devices, shifted(): return lax.ppermute(x, axis, [((i + offset) % n, i) for i in range(n)])  37.3 us
    ppermute x21, waiting for transfers between devices, shifted(): return lax.ppermute(x, axis, [((i + offset) % n, i) for i in range(n)])  27.2 us
    pallas_call x2, Pallas kernels, losses(): pl.pallas_call(functools.partial(loss_kernel, blocks=len(pieces), wide=51...  23 us
    all_to_all x1, blocking collectives, per_device(): got = lax.all_to_all(payload, ('x', 'y', 'z'), 0, 0, tiled=True)[:, 0]  20.7 us
    all_to_all x1, waiting for transfers between devices, per_device(): stream = lax.all_to_all(stream, 'z', 0, 0, tiled=True)  12.3 us
    all_to_all x1, waiting for transfers between devices, per_device(): lax.all_to_all(context, 'z', 0, 0, tiled=True).reshape(nz * samp, -1)  11.6 us
    all_to_all x1, starting transfers between devices, per_device(): lax.all_to_all(context, 'z', 0, 0, tiled=True).reshape(nz * samp, -1)  8.48 us
    pallas_call x1, Pallas kernels, attention(): pl.pallas_call(attention_kernel, out_shape=jax.ShapeDtypeStruct((copies,...  5.61 us
  transfers between devices with their start and end apart: 23, of which 12 were waited for; matrix products, arithmetic and copies ran while one was open for 3% of the time, Pallas kernels for 11%

profile of v2, /device:TPU:8, one launch (start us, length us, event | category | flops | bytes accessed | tf_op | source)
XLA Modules:
  0.0 159.1 jit_solution(6913918871105240372)
XLA Ops:
  0.8 5.6 %attend.1 = bf16[8,16,1024]{2,1,0:T(8,128)(2,1)} custom-call(s32[16]{0:T(128)} %lengths_ref.1, bf16[16,1024]{1,0:T(8,128)(2,1)} %q_ref.1, bf16[16,512]{1,0:T(8,128)(2,1)} %nk_ref.1, bf16[16,512]{1,0:T(8,128)(2,1)} %nv_ref.1, bf16[16,4,128,128]{3,2,1,0:T(8,128)(2,1)} %k_hbm.1, bf16[16,4,128,128]{3,2,1,0:T(8,128)(2,1)} %v_hbm.1), custom_call_target="tpu_custom_call" | custom-call | flops 4294967296 | bytes 4194304 | tf_op jit(solution)/shard_map/attend/pallas_call | solution.py:89
  6.6 2.2 %collective-permute-start.1 = (bf16[72,1152]{1,0:T(8,128)(2,1)S(1)}, bf16[72,1152]{1,0:T(8,128)(2,1)S(1)}, u32[]{:S(2)}, u32[]{:S(2)}) collective-permute-start(bf16[72,1152]{1,0:T(8,128)(2,1)S(1)} %get-tuple-element.23), channel_id=1, source_target_pairs={{16,0},{32,16},{48,32},{0,48},{17,1},{33,17},{49,33},{1,49},{18,2}... | collective-permute-start | bytes 497672 | tf_op jit(solution)/shard_map/ppermute | solution.py:21
  9.7 1.9 %collective-permute-start.3 = (bf16[72,1152]{1,0:T(8,128)(2,1)S(1)}, bf16[72,1152]{1,0:T(8,128)(2,1)S(1)}, u32[]{:S(2)}, u32[]{:S(2)}) collective-permute-start(bf16[72,1152]{1,0:T(8,128)(2,1)S(1)} %get-tuple-element.22), channel_id=1, source_target_pairs={{48,0},{0,16},{16,32},{32,48},{49,1},{1,17},{17,33},{33,49},{50,2}... | collective-permute-start | bytes 497672 | tf_op jit(solution)/shard_map/ppermute | solution.py:21
  11.6 1.8 %collective-permute-done.1 = bf16[72,1152]{1,0:T(8,128)(2,1)S(1)} collective-permute-done((bf16[72,1152]{1,0:T(8,128)(2,1)S(1)}, bf16[72,1152]{1,0:T(8,128)(2,1)S(1)}, u32[]{:S(2)}, u32[]{:S(2)}) %collective-permute-start.1) | collective-permute-done | bytes 165920 | tf_op jit(solution)/shard_map/ppermute | solution.py:21
  13.5 4.3 %collective-permute-done.2 = bf16[72,1152]{1,0:T(8,128)(2,1)S(1)} collective-permute-done((bf16[72,1152]{1,0:T(8,128)(2,1)S(1)}, bf16[72,1152]{1,0:T(8,128)(2,1)S(1)}, u32[]{:S(2)}, u32[]{:S(2)}) %collective-permute-start.2) | collective-permute-done | bytes 165920 | tf_op jit(solution)/shard_map/ppermute | solution.py:21
  18.9 8.5 %all-to-all-start = ((bf16[8,16,1024]{2,1,0:T(8,128)(2,1)}), bf16[8,16,1024]{2,1,0:T(8,128)(2,1)S(1)}, u32[]{:S(2)}, u32[]{:S(2)}) async-start(bf16[8,16,1024]{2,1,0:T(8,128)(2,1)} %attend.1), calls=%async_computation | async-start | bytes 524288 | tf_op jit(solution)/shard_map/all_to_all | solution.py:260
  28.3 11.6 %all-to-all-done = bf16[8,16,1024]{2,1,0:T(8,128)(2,1)S(1)} async-done(((bf16[8,16,1024]{2,1,0:T(8,128)(2,1)}), bf16[8,16,1024]{2,1,0:T(8,128)(2,1)S(1)}, u32[]{:S(2)}, u32[]{:S(2)}) %all-to-all-start) | async-done | bytes 262176 | tf_op jit(solution)/shard_map/all_to_all | solution.py:260
  40.5 1.6 collective-permute-start.5
  42.0 2.7 %collective-permute-start.6 = (f32[32,576]{1,0:T(8,128)S(1)}, f32[32,576]{1,0:T(8,128)S(1)}, u32[]{:S(2)}, u32[]{:S(2)}) collective-permute-start(f32[32,576]{1,0:T(8,128)S(1)} %get-tuple-element.17), channel_id=1, source_target_pairs={{128,0},{192,64},{0,128},{64,192},{129,1},{193,65},{1,129},{65,193... | collective-permute-start | bytes 221192 | tf_op jit(solution)/shard_map/ppermute | solution.py:21
  46.3 2.6 %collective-permute-done.6.c_ref = f32[32,576]{1,0:T(8,128)S(1)} collective-permute-done((f32[32,576]{1,0:T(8,128)S(1)}, f32[32,576]{1,0:T(8,128)S(1)}, u32[]{:S(2)}, u32[]{:S(2)}) %collective-permute-start.6) | collective-permute-done | bytes 73760 | tf_op jit(solution)/shard_map/ppermute | solution.py:21
  50.6 3.4 %all-to-all-start.1 = ((bf16[8,32,576]{2,1,0:T(8,128)(2,1)}), bf16[8,32,576]{2,1,0:T(8,128)(2,1)S(1)}, u32[]{:S(2)}, u32[]{:S(2)}) async-start(bf16[8,32,576]{2,1,0:T(8,128)(2,1)} %stream.1), calls=%async_computation.1 | async-start | bytes 655360 | tf_op jit(solution)/shard_map/all_to_all | solution.py:282
  54.2 12.3 %all-to-all-done.1.got_ref = bf16[8,32,576]{2,1,0:T(8,128)(2,1)S(1)} async-done(((bf16[8,32,576]{2,1,0:T(8,128)(2,1)}), bf16[8,32,576]{2,1,0:T(8,128)(2,1)S(1)}, u32[]{:S(2)}, u32[]{:S(2)}) %all-to-all-start.1) | async-done | bytes 294944 | tf_op jit(solution)/shard_map/all_to_all | solution.py:282
  67.6 3.2 %collective-permute-start.9 = (bf16[16,4736]{1,0:T(8,128)(2,1)S(1)}, bf16[16,4736]{1,0:T(8,128)(2,1)S(1)}, u32[]{:S(2)}, u32[]{:S(2)}) collective-permute-start(bf16[16,4736]{1,0:T(8,128)(2,1)S(1)} %get-tuple-element.21), channel_id=1, source_target_pairs={{128,0},{192,64},{0,128},{64,192},{129,1},{193,65},{1,129},{65,193... | collective-permute-start | bytes 454664 | tf_op jit(solution)/shard_map/ppermute | solution.py:21
  72.1 1.5 collective-permute-start.13
  73.7 3.4 %collective-permute-start.12 = (bf16[16,4736]{1,0:T(8,128)(2,1)S(1)}, bf16[16,4736]{1,0:T(8,128)(2,1)S(1)}, u32[]{:S(2)}, u32[]{:S(2)}) collective-permute-start(bf16[16,4736]{1,0:T(8,128)(2,1)S(1)} %get-tuple-element.20), channel_id=1, source_target_pairs={{32,0},{48,16},{0,32},{16,48},{33,1},{49,17},{1,33},{17,49},{34,2}... | collective-permute-start | bytes 454664 | tf_op jit(solution)/shard_map/ppermute | solution.py:21
  79.5 2.5 %collective-permute-done.12 = bf16[16,4736]{1,0:T(8,128)(2,1)S(1)} collective-permute-done((bf16[16,4736]{1,0:T(8,128)(2,1)S(1)}, bf16[16,4736]{1,0:T(8,128)(2,1)S(1)}, u32[]{:S(2)}, u32[]{:S(2)}) %collective-permute-start.12) | collective-permute-done | bytes 151584 | tf_op jit(solution)/shard_map/ppermute | solution.py:21
  82.0 2.7 %collective-permute-done.11 = bf16[16,4736]{1,0:T(8,128)(2,1)} collective-permute-done((bf16[16,4736]{1,0:T(8,128)(2,1)S(1)}, bf16[16,4736]{1,0:T(8,128)(2,1)}, u32[]{:S(2)}, u32[]{:S(2)}) %collective-permute-start.11) | collective-permute-done | bytes 151584 | tf_op jit(solution)/shard_map/ppermute | solution.py:21
  84.7 2.7 %collective-permute-start.16 = (bf16[64,4736]{1,0:T(8,128)(2,1)S(1)}, bf16[64,4736]{1,0:T(8,128)(2,1)S(1)}, u32[]{:S(2)}, u32[]{:S(2)}) collective-permute-start(bf16[64,4736]{1,0:T(8,128)(2,1)S(1)} %pad_maximum_fusion.refs_4_), channel_id=1, source_target_pairs={{32,0},{48,16},{0,32},{16,48},{33,1},{49,17},{1,33},{17,49},{34,2}... | collective-permute-start | bytes 1818632 | tf_op jit(solution)/shard_map/ppermute | solution.py:21
  89.1 9.1 %collective-permute-done.14.refs_4_ = bf16[64,4736]{1,0:T(8,128)(2,1)S(1)} collective-permute-done((bf16[64,4736]{1,0:T(8,128)(2,1)S(1)}, bf16[64,4736]{1,0:T(8,128)(2,1)S(1)}, u32[]{:S(2)}, u32[]{:S(2)}) %collective-permute-start.14) | collective-permute-done | bytes 606240 | tf_op jit(solution)/shard_map/ppermute | solution.py:21
  99.0 10.0 %collective-permute-start.19 = (bf16[64,4736]{1,0:T(8,128)(2,1)S(1)}, bf16[64,4736]{1,0:T(8,128)(2,1)}, u32[]{:S(2)}, u32[]{:S(2)}) collective-permute-start(bf16[64,4736]{1,0:T(8,128)(2,1)S(1)} %pad_maximum_fusion.1.refs_5_), channel_id=1, source_target_pairs={{128,0},{192,64},{0,128},{64,192},{129,1},{193,65},{1,129},{65,193... | collective-permute-start | bytes 1818632 | tf_op jit(solution)/shard_map/ppermute | solution.py:21
  110.1 10.4 %shard_map.149 = f32[8,128]{1,0:T(8,128)S(1)} custom-call(s32[2]{0:T(128)S(1)} %pad_add_fusion.refs_0_, s32[128,1]{1,0:T(8,128)S(1)} %copy.47.refs_1_, bf16[1000,4608]{1,0:T(8,128)(2,1)} %collective-permute-done.refs_2_, bf16[1000,4608]{1,0:T(8,128)(2,1)} %refs_3_.3, bf16[64,4736]{1,0:T(8,128)(2,1)S(1)} %pad_maximum_fusion.refs_4_, ...), custom_call_target="tpu_custom_call" | custom-call | flops 2359296000 | bytes 18432000 | tf_op jit(solution)/shard_map/pallas_call | solution.py:194
  120.7 3.0 %collective-permute-done.19.refs_9_ = bf16[64,4736]{1,0:T(8,128)(2,1)} collective-permute-done((bf16[64,4736]{1,0:T(8,128)(2,1)S(1)}, bf16[64,4736]{1,0:T(8,128)(2,1)}, u32[]{:S(2)}, u32[]{:S(2)}) %collective-permute-start.19) | collective-permute-done | bytes 606240 | tf_op jit(solution)/shard_map/ppermute | solution.py:21
  123.7 12.6 %shard_map.150 = f32[8,384]{1,0:T(8,128)S(1)} custom-call(s32[2]{0:T(128)S(1)} %pad_add_fusion.refs_0_, s32[384,1]{1,0:T(8,128)S(1)} %reshape.82.refs_1_, bf16[1000,4608]{1,0:T(8,128)(2,1)} %collective-permute-done.refs_2_, bf16[1000,4608]{1,0:T(8,128)(2,1)} %refs_3_.3, bf16[64,4736]{1,0:T(8,128)(2,1)S(1)} %collective-permute-done.14.refs_4_, ...), custom_call_target="tpu_custom_call" | custom-call | flops 7077888000 | bytes 18432000 | tf_op jit(solution)/shard_map/pallas_call | solution.py:194
  137.5 20.7 %all_to_all.15 = f32[128,1,256]{2,1,0:T(1,128)S(1)} all-to-all(f32[128,1,256]{2,1,0:T(1,128)S(1)} %broadcast_in_dim.50), channel_id=1, replica_groups=mesh['x'=4,'y'=4,'z'=8,'c'=2] {'x','y','z'}, dimensions={0} | all-to-all | bytes 262144 | tf_op jit(solution)/shard_map/all_to_all | solution.py:329
  (120 shorter events, 17.4 us)
Async XLA Ops:
  0.6 98.4 %collective-permute-start = (bf16[1000,4608]{1,0:T(8,128)(2,1)}, bf16[1000,4608]{1,0:T(8,128)(2,1)}, u32[]{:S(2)}, u32[]{:S(2)}) collective-permute-start(bf16[1000,4608]{1,0:T(8,128)(2,1)} %refs_3_.3), channel_id=1, source_target_pairs={{1,0},{0,1},{3,2},{2,3},{5,4},{4,5},{7,6},{6,7},{9,8},{8,9},{11,10... | collective-permute-start | bytes 27648008 | tf_op jit(solution)/shard_map/ppermute | solution.py:21
  6.6 6.9 %collective-permute-start.1 = (bf16[72,1152]{1,0:T(8,128)(2,1)S(1)}, bf16[72,1152]{1,0:T(8,128)(2,1)S(1)}, u32[]{:S(2)}, u32[]{:S(2)}) collective-permute-start(bf16[72,1152]{1,0:T(8,128)(2,1)S(1)} %get-tuple-element.23), channel_id=1, source_target_pairs={{16,0},{32,16},{48,32},{0,48},{17,1},{33,17},{49,33},{1,49},{18,2}... | collective-permute-start | bytes 497672 | tf_op jit(solution)/shard_map/ppermute | solution.py:21
  8.8 8.9 %collective-permute-start.2 = (bf16[72,1152]{1,0:T(8,128)(2,1)S(1)}, bf16[72,1152]{1,0:T(8,128)(2,1)S(1)}, u32[]{:S(2)}, u32[]{:S(2)}) collective-permute-start(bf16[72,1152]{1,0:T(8,128)(2,1)S(1)} %get-tuple-element.24), channel_id=1, source_target_pairs={{32,0},{48,16},{0,32},{16,48},{33,1},{49,17},{1,33},{17,49},{34,2}... | collective-permute-start | bytes 497672 | tf_op jit(solution)/shard_map/ppermute | solution.py:21
  9.7 8.8 %collective-permute-start.3 = (bf16[72,1152]{1,0:T(8,128)(2,1)S(1)}, bf16[72,1152]{1,0:T(8,128)(2,1)S(1)}, u32[]{:S(2)}, u32[]{:S(2)}) collective-permute-start(bf16[72,1152]{1,0:T(8,128)(2,1)S(1)} %get-tuple-element.22), channel_id=1, source_target_pairs={{48,0},{0,16},{16,32},{32,48},{49,1},{1,17},{17,33},{33,49},{50,2}... | collective-permute-start | bytes 497672 | tf_op jit(solution)/shard_map/ppermute | solution.py:21
  18.8 9.0 %collective-permute-start.4 = (bf16[4,72,1152]{2,1,0:T(8,128)(2,1)S(1)}, bf16[4,72,1152]{2,1,0:T(8,128)(2,1)S(1)}, u32[]{:S(2)}, u32[]{:S(2)}) collective-permute-start(bf16[4,72,1152]{2,1,0:T(8,128)(2,1)S(1)} %constant_dynamic-slice_fusion.1), channel_id=1, source_target_pairs={{1,0},{0,1},{3,2},{2,3},{5,4},{4,5},{7,6},{6,7},{9,8},{8,9},{11,10... | collective-permute-start | bytes 1990664 | tf_op jit(solution)/shard_map/ppermute | solution.py:21
  18.9 21.0 %all-to-all-start = ((bf16[8,16,1024]{2,1,0:T(8,128)(2,1)}), bf16[8,16,1024]{2,1,0:T(8,128)(2,1)S(1)}, u32[]{:S(2)}, u32[]{:S(2)}) async-start(bf16[8,16,1024]{2,1,0:T(8,128)(2,1)} %attend.1), calls=%async_computation | async-start | bytes 524288 | tf_op jit(solution)/shard_map/all_to_all | solution.py:260
  40.5 5.8 %collective-permute-start.5 = (f32[32,576]{1,0:T(8,128)S(1)}, f32[32,576]{1,0:T(8,128)S(1)}, u32[]{:S(2)}, u32[]{:S(2)}) collective-permute-start(f32[32,576]{1,0:T(8,128)S(1)} %get-tuple-element.18), channel_id=1, source_target_pairs={{192,0},{0,64},{64,128},{128,192},{193,1},{1,65},{65,129},{129,193... | collective-permute-start | bytes 221192 | tf_op jit(solution)/shard_map/ppermute | solution.py:21
  42.0 6.9 %collective-permute-start.6 = (f32[32,576]{1,0:T(8,128)S(1)}, f32[32,576]{1,0:T(8,128)S(1)}, u32[]{:S(2)}, u32[]{:S(2)}) collective-permute-start(f32[32,576]{1,0:T(8,128)S(1)} %get-tuple-element.17), channel_id=1, source_target_pairs={{128,0},{192,64},{0,128},{64,192},{129,1},{193,65},{1,129},{65,193... | collective-permute-start | bytes 221192 | tf_op jit(solution)/shard_map/ppermute | solution.py:21
  44.8 4.4 %collective-permute-start.7 = (f32[32,576]{1,0:T(8,128)S(1)}, f32[32,576]{1,0:T(8,128)S(1)}, u32[]{:S(2)}, u32[]{:S(2)}) collective-permute-start(f32[32,576]{1,0:T(8,128)S(1)} %get-tuple-element.16), channel_id=1, source_target_pairs={{64,0},{128,64},{192,128},{0,192},{65,1},{129,65},{193,129},{1,193... | collective-permute-start | bytes 221192 | tf_op jit(solution)/shard_map/ppermute | solution.py:21
  49.2 22.8 %copy-start.6 = (s32[16]{0:T(128)S(1)}, s32[16]{0:T(128)}, u32[]{:S(2)}) copy-start(s32[16]{0:T(128)} %param.27) | copy-start | bytes 196
  50.6 15.9 %all-to-all-start.1 = ((bf16[8,32,576]{2,1,0:T(8,128)(2,1)}), bf16[8,32,576]{2,1,0:T(8,128)(2,1)S(1)}, u32[]{:S(2)}, u32[]{:S(2)}) async-start(bf16[8,32,576]{2,1,0:T(8,128)(2,1)} %stream.1), calls=%async_computation.1 | async-start | bytes 655360 | tf_op jit(solution)/shard_map/all_to_all | solution.py:282
  66.9 6.8 %collective-permute-start.10 = (bf16[16,4736]{1,0:T(8,128)(2,1)S(1)}, bf16[16,4736]{1,0:T(8,128)(2,1)S(1)}, u32[]{:S(2)}, u32[]{:S(2)}) collective-permute-start(bf16[16,4736]{1,0:T(8,128)(2,1)S(1)} %get-tuple-element.21), channel_id=1, source_target_pairs={{192,0},{0,64},{64,128},{128,192},{193,1},{1,65},{65,129},{129,193... | collective-permute-start | bytes 454664 | tf_op jit(solution)/shard_map/ppermute | solution.py:21
  67.6 9.5 %collective-permute-start.9 = (bf16[16,4736]{1,0:T(8,128)(2,1)S(1)}, bf16[16,4736]{1,0:T(8,128)(2,1)S(1)}, u32[]{:S(2)}, u32[]{:S(2)}) collective-permute-start(bf16[16,4736]{1,0:T(8,128)(2,1)S(1)} %get-tuple-element.21), channel_id=1, source_target_pairs={{128,0},{192,64},{0,128},{64,192},{129,1},{193,65},{1,129},{65,193... | collective-permute-start | bytes 454664 | tf_op jit(solution)/shard_map/ppermute | solution.py:21
  70.8 7.7 %collective-permute-start.8 = (bf16[16,4736]{1,0:T(8,128)(2,1)S(1)}, bf16[16,4736]{1,0:T(8,128)(2,1)S(1)}, u32[]{:S(2)}, u32[]{:S(2)}) collective-permute-start(bf16[16,4736]{1,0:T(8,128)(2,1)S(1)} %get-tuple-element.21), channel_id=1, source_target_pairs={{64,0},{128,64},{192,128},{0,192},{65,1},{129,65},{193,129},{1,193... | collective-permute-start | bytes 454664 | tf_op jit(solution)/shard_map/ppermute | solution.py:21
  72.1 7.3 %collective-permute-start.13 = (bf16[16,4736]{1,0:T(8,128)(2,1)S(1)}, bf16[16,4736]{1,0:T(8,128)(2,1)S(1)}, u32[]{:S(2)}, u32[]{:S(2)}) collective-permute-start(bf16[16,4736]{1,0:T(8,128)(2,1)S(1)} %get-tuple-element.20), channel_id=1, source_target_pairs={{48,0},{0,16},{16,32},{32,48},{49,1},{1,17},{17,33},{33,49},{50,2}... | collective-permute-start | bytes 454664 | tf_op jit(solution)/shard_map/ppermute | solution.py:21
  73.7 8.3 %collective-permute-start.12 = (bf16[16,4736]{1,0:T(8,128)(2,1)S(1)}, bf16[16,4736]{1,0:T(8,128)(2,1)S(1)}, u32[]{:S(2)}, u32[]{:S(2)}) collective-permute-start(bf16[16,4736]{1,0:T(8,128)(2,1)S(1)} %get-tuple-element.20), channel_id=1, source_target_pairs={{32,0},{48,16},{0,32},{16,48},{33,1},{49,17},{1,33},{17,49},{34,2}... | collective-permute-start | bytes 454664 | tf_op jit(solution)/shard_map/ppermute | solution.py:21
  77.1 7.6 %collective-permute-start.11 = (bf16[16,4736]{1,0:T(8,128)(2,1)S(1)}, bf16[16,4736]{1,0:T(8,128)(2,1)}, u32[]{:S(2)}, u32[]{:S(2)}) collective-permute-start(bf16[16,4736]{1,0:T(8,128)(2,1)S(1)} %get-tuple-element.20), channel_id=1, source_target_pairs={{16,0},{32,16},{48,32},{0,48},{17,1},{33,17},{49,33},{1,49},{18,2}... | collective-permute-start | bytes 454664 | tf_op jit(solution)/shard_map/ppermute | solution.py:21
  78.6 19.7 %collective-permute-start.14 = (bf16[64,4736]{1,0:T(8,128)(2,1)S(1)}, bf16[64,4736]{1,0:T(8,128)(2,1)S(1)}, u32[]{:S(2)}, u32[]{:S(2)}) collective-permute-start(bf16[64,4736]{1,0:T(8,128)(2,1)S(1)} %pad_maximum_fusion.refs_4_), channel_id=1, source_target_pairs={{16,0},{32,16},{48,32},{0,48},{17,1},{33,17},{49,33},{1,49},{18,2}... | collective-permute-start | bytes 1818632 | tf_op jit(solution)/shard_map/ppermute | solution.py:21
  79.4 8.9 %collective-permute-start.20 = (f32[128]{0:T(128)S(1)}, f32[128]{0:T(128)S(1)}, u32[]{:S(2)}, u32[]{:S(2)}) collective-permute-start(f32[128]{0:T(128)S(1)} %select_reduce_fusion.1), channel_id=1, source_target_pairs={{1,0},{0,1},{3,2},{2,3},{5,4},{4,5},{7,6},{6,7},{9,8},{8,9},{11,10... | collective-permute-start | bytes 1544 | tf_op jit(solution)/shard_map/ppermute | solution.py:21
  82.0 38.7 %collective-permute-start.15 = (bf16[64,4736]{1,0:T(8,128)(2,1)S(1)}, bf16[64,4736]{1,0:T(8,128)(2,1)S(1)}, u32[]{:S(2)}, u32[]{:S(2)}) collective-permute-start(bf16[64,4736]{1,0:T(8,128)(2,1)S(1)} %pad_maximum_fusion.refs_4_), channel_id=1, source_target_pairs={{48,0},{0,16},{16,32},{32,48},{49,1},{1,17},{17,33},{33,49},{50,2}... | collective-permute-start | bytes 1818632 | tf_op jit(solution)/shard_map/ppermute | solution.py:21
  84.7 36.0 %collective-permute-start.16 = (bf16[64,4736]{1,0:T(8,128)(2,1)S(1)}, bf16[64,4736]{1,0:T(8,128)(2,1)S(1)}, u32[]{:S(2)}, u32[]{:S(2)}) collective-permute-start(bf16[64,4736]{1,0:T(8,128)(2,1)S(1)} %pad_maximum_fusion.refs_4_), channel_id=1, source_target_pairs={{32,0},{48,16},{0,32},{16,48},{33,1},{49,17},{1,33},{17,49},{34,2}... | collective-permute-start | bytes 1818632 | tf_op jit(solution)/shard_map/ppermute | solution.py:21
  88.4 32.3 %collective-permute-start.17 = (bf16[64,4736]{1,0:T(8,128)(2,1)S(1)}, bf16[64,4736]{1,0:T(8,128)(2,1)}, u32[]{:S(2)}, u32[]{:S(2)}) collective-permute-start(bf16[64,4736]{1,0:T(8,128)(2,1)S(1)} %pad_maximum_fusion.1.refs_5_), channel_id=1, source_target_pairs={{64,0},{128,64},{192,128},{0,192},{65,1},{129,65},{193,129},{1,193... | collective-permute-start | bytes 1818632 | tf_op jit(solution)/shard_map/ppermute | solution.py:21
  98.2 22.5 %collective-permute-start.18 = (bf16[64,4736]{1,0:T(8,128)(2,1)S(1)}, bf16[64,4736]{1,0:T(8,128)(2,1)}, u32[]{:S(2)}, u32[]{:S(2)}) collective-permute-start(bf16[64,4736]{1,0:T(8,128)(2,1)S(1)} %pad_maximum_fusion.1.refs_5_), channel_id=1, source_target_pairs={{192,0},{0,64},{64,128},{128,192},{193,1},{1,65},{65,129},{129,193... | collective-permute-start | bytes 1818632 | tf_op jit(solution)/shard_map/ppermute | solution.py:21
  99.0 24.7 %collective-permute-start.19 = (bf16[64,4736]{1,0:T(8,128)(2,1)S(1)}, bf16[64,4736]{1,0:T(8,128)(2,1)}, u32[]{:S(2)}, u32[]{:S(2)}) collective-permute-start(bf16[64,4736]{1,0:T(8,128)(2,1)S(1)} %pad_maximum_fusion.1.refs_5_), channel_id=1, source_target_pairs={{128,0},{192,64},{0,128},{64,192},{129,1},{193,65},{1,129},{65,193... | collective-permute-start | bytes 1818632 | tf_op jit(solution)/shard_map/ppermute | solution.py:21
  (6 other events, 73.9 us)
